TPU v7x, 8 devices: a whole 2x2x1 slice. The times are simulated.
8 devices in a mesh: dp: 1 (over z), tp: 2 (over y), sp: 4 (over x, core).
Axes of the slice: x: 2, y: 2, z: 1, core: 2. Of those that a mesh axis runs over, the one named last changes fastest.
Arguments:
- x_in: bfloat16 [512, 2304], P('dp')
- cur_pos: int32 [512], P('dp')
- w_pre: float32 [2304], replicated
- w_q: bfloat16 [2304, 2048], P(None, 'tp')
- w_k: bfloat16 [2304, 1024], P(None, 'tp')
- w_v: bfloat16 [2304, 1024], P(None, 'tp')
- w_o: bfloat16 [2048, 2304], P('tp')
- w_post: float32 [2304], replicated
- k_cache: bfloat16 [512, 256, 4, 256], P('dp', 'sp', 'tp')
- v_cache: bfloat16 [512, 256, 4, 256], P('dp', 'sp', 'tp')
Outputs:
- output 1: bfloat16 [512, 2304], P('dp')
- output 2: bfloat16 [512, 256, 4, 256], P('dp', 'sp', 'tp')
- output 3: bfloat16 [512, 256, 4, 256], P('dp', 'sp', 'tp')
All inputs are finite; a program needn't handle non-finite values.
Results may differ from a plain program's by a relative error of at most 0.00629532.
Values sent between devices are 32-bit elements.
A program may use at most 1 GiB of HBM per device.

v0:
```python
import jax
import jax.numpy as jnp
from jax import lax
from jax.sharding import PartitionSpec as P

SOFT_CAP = 50.0
ROPE_BASE = 10000.0
NORM_EPS = 1e-6
NEG_FILL = -1e30


def rms_scale(tensor, gain_w):
    mean_sq = jnp.mean(tensor * tensor, axis=-1, keepdims=True)
    return tensor * lax.rsqrt(mean_sq + NORM_EPS) * (1.0 + gain_w)


def rotary(tensor, positions):
    half_dim = tensor.shape[-1] // 2
    inv_freq = ROPE_BASE ** (-2.0 * jnp.arange(half_dim, dtype=jnp.float32) / (2 * half_dim))
    angles = positions.astype(jnp.float32)[:, None] * inv_freq[None, :]
    angles = angles.reshape((angles.shape[0],) + (1,) * (tensor.ndim - 2) + (half_dim,))
    cos_tab = jnp.cos(angles)
    sin_tab = jnp.sin(angles)
    lo_half = tensor[..., :half_dim]
    hi_half = tensor[..., half_dim:]
    return jnp.concatenate([lo_half * cos_tab - hi_half * sin_tab, hi_half * cos_tab + lo_half * sin_tab], axis=-1)


def solution(mesh):
    cache_spec = P('dp', 'sp', 'tp', None)

    def local_step(x_in, cur_pos, w_pre, w_q, w_k, w_v, w_o, w_post, k_cache, v_cache):
        row_count, seq_block, kv_local, head_dim = k_cache.shape
        heads_local = w_q.shape[1] // head_dim
        group_size = heads_local // kv_local
        sp_index = lax.axis_index('sp')
        normed = rms_scale(x_in.astype(jnp.float32), w_pre).astype(jnp.bfloat16)
        q_proj = jnp.dot(normed, w_q, preferred_element_type=jnp.float32)
        q_rot = rotary(q_proj.reshape(row_count, kv_local, group_size, head_dim), cur_pos).astype(jnp.bfloat16)
        k_proj = jnp.dot(normed, w_k, preferred_element_type=jnp.float32)
        k_new = rotary(k_proj.reshape(row_count, kv_local, head_dim), cur_pos).astype(jnp.bfloat16)
        v_new = jnp.dot(normed, w_v, preferred_element_type=jnp.float32).reshape(row_count, kv_local, head_dim).astype(jnp.bfloat16)
        block_pos = sp_index * seq_block + jnp.arange(seq_block)
        slot_hit = (block_pos[None, :] == cur_pos[:, None])[:, :, None, None]
        k_out = jnp.where(slot_hit, k_new[:, None], k_cache)
        v_out = jnp.where(slot_hit, v_new[:, None], v_cache)
        raw_score = jnp.einsum('bgrd,btgd->bgrt', q_rot, k_out, preferred_element_type=jnp.float32)
        capped = SOFT_CAP * jnp.tanh(raw_score * (head_dim ** -0.5 / SOFT_CAP))
        is_valid = (block_pos[None, :] <= cur_pos[:, None])[:, None, None, :]
        capped = jnp.where(is_valid, capped, NEG_FILL)
        block_max = jnp.max(capped, axis=-1)
        exp_w = jnp.where(is_valid, jnp.exp(capped - block_max[..., None]), 0.0)
        block_sum = jnp.sum(exp_w, axis=-1)
        block_out = jnp.einsum('bgrt,btgd->bgrd', exp_w.astype(jnp.bfloat16), v_out, preferred_element_type=jnp.float32)
        global_max = lax.pmax(block_max, 'sp')
        factor = jnp.exp(block_max - global_max)
        packed = jnp.concatenate([block_out * factor[..., None], (block_sum * factor)[..., None]], axis=-1)
        merged = lax.psum(packed, 'sp')
        attn_out = (merged[..., :head_dim] / merged[..., head_dim:]).reshape(row_count, heads_local * head_dim)
        proj_part = jnp.dot(attn_out.astype(jnp.bfloat16), w_o, preferred_element_type=jnp.float32)
        proj_sum = lax.psum(proj_part, 'tp')
        x_out = (x_in.astype(jnp.float32) + rms_scale(proj_sum, w_post)).astype(jnp.bfloat16)
        return x_out, k_out, v_out

    return jax.shard_map(local_step, mesh=mesh,
                         in_specs=(P('dp', None), P('dp'), P(None), P(None, 'tp'), P(None, 'tp'), P(None, 'tp'), P('tp', None), P(None), cache_spec, cache_spec),
                         out_specs=(P('dp', None), cache_spec, cache_spec), check_vma=False)
```

profile of v0, /device:TPU:0, one launch (start us, length us, event | category | flops | bytes accessed | tf_op | source)
XLA Modules:
  0.0 406.0 jit_solution(11506913218409788132)
XLA Ops:
  7.2 0.0 copy-start
  7.2 0.0 all-reduce.3.cloned.1.call-start
  7.2 0.9 broadcast_add_fusion.1
  8.1 2.2 fusion.4
  10.3 0.0 copy-start.8
  10.3 0.7 convert_element_type.41
  11.0 1.0 multiply_cosine_fusion
  12.0 0.1 copy.30
  12.1 0.1 copy.31
  12.3 0.0 copy-done
  12.3 3.2 fusion.33
  15.5 0.2 subtract_convert_fusion.1
  15.7 0.6 copy.32
  16.4 0.0 copy-done.8
  16.4 0.0 copy-start.7
  16.4 0.0 copy-start.3
  16.4 4.8 %convolution_convert_fusion = bf16[512,512]{0,1:T(8,128)(2,1)} fusion(bf16[2304,512]{1,0:T(8,128)(2,1)} %param.15, bf16[512,2304]{1,0:T(8,128)(2,1)} %param.10, f32[2304]{0:T(1024)S(1)} %broadcast_add_fusion.1, f32[512]{0:T(512)S(1)} %add_rsqrt_fusion.1), kind=kOutput, calls=%fused_computation.18 | convolution fusion | flops 1212940288 | bytes 5254144 | tf_op jit(solution)/shard_map/dot_general | solution.py:42
  21.3 2.0 copy.34
  23.2 0.0 copy-done.7
  23.2 0.1 broadcast_compare_fusion
  23.4 0.0 copy-done.3
  23.4 6.3 %fusion.35 = f32[512,1024]{1,0:T(8,128)} fusion(bf16[2304,1024]{1,0:T(8,128)(2,1)} %param.13, bf16[512,2304]{1,0:T(8,128)(2,1)S(1)} %copy-done.3, f32[2304]{0:T(1024)S(1)} %broadcast_add_fusion.1, f32[512]{0:T(512)} %copy-done.8), kind=kOutput, calls=%fused_computation.49 | convolution fusion | flops 2420637696 | bytes 9186304 | tf_op jit(solution)/shard_map/dot_general | solution.py:38
  29.7 3.0 reshape.208
  32.8 1.9 subtract_convert_fusion
  34.7 83.9 %broadcast_select_fusion = (bf16[512,64,2,256]{3,2,1,0:T(2,128)(2,1)}, bf16[512,64,2,256]{3,2,1,0:T(2,128)(2,1)}) fusion(bf16[512,64,2,256]{3,2,1,0:T(2,128)(2,1)} %param.19, pred[512,64]{1,0:T(8,128)(4,1)S(1)} %get-tuple-element.13, bf16[512,2,256]{2,1,0:T(2,128)(2,1)} %copy.34, bf16[512,64,2,256]{3,2,1,0:T(2,128)(2,1)} %param.18, ...), kind=kLoop, calls=%fused_computation | loop fusion | flops 33554432 | bytes 135299072 | tf_op jit(solution)/shard_map/jit(_where)/select_n | solution.py:46
  118.6 0.0 copy-done.4
  118.6 0.0 copy-done.5
  118.6 16.3 %fusion.37 = (f32[512,2,2]{2,1,0:T(2,128)S(1)}, f32[512,2,2,64]{3,2,1,0:T(2,128)S(1)}) fusion(bf16[512,64,2,256]{3,2,1,0:T(2,128)(2,1)} %get-tuple-element.10, bf16[512,2,2,128]{3,2,1,0:T(2,128)(2,1)S(1)} %copy-done.5, bf16[512,2,2,128]{3,2,1,0:T(2,128)(2,1)S(1)} %copy-done.4, pred[512,64]{1,0:T(8,128)(4,1)S(1)} %get-tuple-element.14), kind=kOutput, calls=%fused_computation.50 | convolution fusion | flops 69728256 | bytes 35168256 | tf_op jit(solution)/shard_map/bgrd,btgd->bgrt/dot_general | solution.py:47
  134.9 18.9 %pmax.7 = f32[512,2,2]{2,1,0:T(2,128)S(1)} all-reduce(f32[512,2,2]{2,1,0:T(2,128)S(1)} %get-tuple-element.15), channel_id=1, replica_groups=mesh['dp'=1,'tp'=2,'sp'=4] {'sp'}, use_global_device_ids=true, to_apply=%region_2.3 | all-reduce | flops 2048 | bytes 16384 | tf_op jit(solution)/shard_map/pmax | solution.py:55
  153.9 14.3 %fusion.29 = f32[512,2,2]{2,1,0:T(2,128)S(1)} fusion(f32[512,2,2,64]{3,2,1,0:T(2,128)S(1)} %get-tuple-element.16, f32[512,2,2]{2,1,0:T(2,128)S(1)} %get-tuple-element.15, pred[512,64]{1,0:T(8,128)(4,1)S(1)} %get-tuple-element.14), kind=kLoop, calls=%fused_computation.39 | loop fusion | flops 391168 | bytes 573440 | tf_op jit(solution)/shard_map/reduce_sum | solution.py:53
  168.2 1.3 multiply_bitcast_fusion
  169.6 6.5 %copy.37 = f32[512,2,2,1]{3,2,1,0:T(2,128)S(1)} copy(f32[512,2,2,1]{2,1,0,3:T(2,128)S(1)} %get-tuple-element.3) | data formatting | bytes 16384 | tf_op jit(solution)/shard_map/broadcast_in_dim | solution.py:57
  176.0 16.3 %fusion.9 = f32[512,2,2,256]{3,2,1,0:T(2,128)S(1)} fusion(bf16[512,64,2,256]{3,2,1,0:T(2,128)(2,1)} %get-tuple-element.9, f32[512,2,2]{2,1,0:T(2,128)} %get-tuple-element.4, f32[512,2,2,64]{3,2,1,0:T(2,128)S(1)} %get-tuple-element.16, pred[512,64]{1,0:T(8,128)(4,1)S(1)} %get-tuple-element.14, f32[512,2,2]{2,1,0:T(2,128)S(1)} %get-tuple-element.15), kind=kOutput, calls=%fused_computation.17 | convolution fusion | flops 68026368 | bytes 36225024 | tf_op jit(solution)/shard_map/bgrt,btgd->bgrd/dot_general | solution.py:54
  192.3 3.2 pad_maximum_fusion
  195.6 0.0 all-reduce.3.cloned.1.call-update
  195.6 0.0 all-reduce.5.cloned.1.call-start
  195.6 63.1 %all-reduce.3.cloned.1.call-done = f32[512,2,2,257]{3,2,1,0:T(2,128)} async-done(((f32[512,2,2,257]{3,2,1,0:T(2,128)}), f32[512,2,2,257]{3,2,1,0:T(2,128)}) %all-reduce.3.cloned.1.call-update) | async-done | bytes 2105360 | tf_op jit(solution)/shard_map/psum | solution.py:58
  258.8 1.6 slice.29
  260.4 6.8 %copy.42 = f32[512,2,2,1]{2,1,0,3:T(2,128)S(1)} copy(f32[512,2,2,1]{3,2,1,0:T(2,128)S(1)} %slice.29) | data formatting | bytes 16384 | tf_op jit(solution)/shard_map/div | solution.py:59
  267.1 3.4 fusion.8
  270.5 0.8 convert_element_type.46
  271.3 6.6 %fusion.38 = f32[512,2304]{1,0:T(8,128)} fusion(bf16[512,1024]{1,0:T(8,128)(2,1)S(1)} %convert_element_type.46, bf16[1024,2304]{1,0:T(8,128)(2,1)} %param.16), kind=kOutput, calls=%fused_computation.51 | convolution fusion | flops 2415919104 | bytes 10485760 | tf_op jit(solution)/shard_map/dot_general | solution.py:60
  277.9 0.0 all-reduce.5.cloned.1.call-update
  277.9 0.7 copy-done.6
  278.6 113.0 %all-reduce.5.cloned.1.call-done = f32[512,2304]{1,0:T(8,128)} async-done(((f32[512,2304]{1,0:T(8,128)}), f32[512,2304]{1,0:T(8,128)}) %all-reduce.5.cloned.1.call-update) | async-done | bytes 4718608 | tf_op jit(solution)/shard_map/psum | solution.py:61
  391.5 2.9 multiply_reduce_fusion
  394.4 0.9 copy-done.2
  395.3 3.9 fusion.7
  (12 shorter events, 0.1 us)
Async XLA Ops:
  7.2 5.1 %copy-start = (bf16[2304,512]{1,0:T(8,128)(2,1)S(1)}, bf16[2304,512]{1,0:T(8,128)(2,1)}, u32[]{:S(2)}) copy-start(bf16[2304,512]{1,0:T(8,128)(2,1)} %param.14) | copy-start | bytes 7077892
  7.2 251.6 %all-reduce.3.cloned.1.call-start = ((), (), s32[]{:S(2)}) async-start(), calls=%async_computation | async-start | bytes 6291456 | tf_op jit(solution)/shard_map/psum | solution.py:58
  10.3 6.1 %copy-start.8 = (f32[512]{0:T(512)}, f32[512]{0:T(512)S(1)}, u32[]{:S(2)}) copy-start(f32[512]{0:T(512)S(1)} %add_rsqrt_fusion.1) | copy-start | bytes 6148
  16.4 6.9 %copy-start.7 = (s32[512]{0:T(512)S(1)}, s32[512]{0:T(512)}, u32[]{:S(2)}) copy-start(s32[512]{0:T(512)} %param.11) | copy-start | bytes 6148
  16.4 7.0 %copy-start.3 = (bf16[512,2304]{1,0:T(8,128)(2,1)S(1)}, bf16[512,2304]{1,0:T(8,128)(2,1)}, u32[]{:S(2)}) copy-start(bf16[512,2304]{1,0:T(8,128)(2,1)} %param.10) | copy-start | bytes 7077892
  34.7 83.9 %copy-start.4 = (bf16[512,2,2,128]{3,2,1,0:T(2,128)(2,1)S(1)}, bf16[512,2,2,128]{3,2,1,0:T(2,128)(2,1)}, u32[]{:S(2)}) copy-start(bf16[512,2,2,128]{3,2,1,0:T(2,128)(2,1)} %get-tuple-element.5) | copy-start | bytes 1572868
  34.7 83.9 %copy-start.5 = (bf16[512,2,2,128]{3,2,1,0:T(2,128)(2,1)S(1)}, bf16[512,2,2,128]{3,2,1,0:T(2,128)(2,1)}, u32[]{:S(2)}) copy-start(bf16[512,2,2,128]{3,2,1,0:T(2,128)(2,1)} %get-tuple-element.6) | copy-start | bytes 1572868
  195.6 196.0 %all-reduce.5.cloned.1.call-start = ((), (), s32[]{:S(2)}) async-start(), calls=%async_computation.1 | async-start | bytes 9437184 | tf_op jit(solution)/shard_map/psum | solution.py:61
  277.9 0.7 copy-start.6
  391.5 3.8 copy-start.2
  394.4 4.8 %copy-start.1 = (bf16[2304,512]{1,0:T(8,128)(2,1)S(1)}, bf16[2304,512]{1,0:T(8,128)(2,1)}, u32[]{:S(2)}) copy-start(bf16[2304,512]{1,0:T(8,128)(2,1)} %param.14) | copy-start | bytes 7077892
Sparse Core Ops, SparseCore 0:
  195.7 63.0 all-reduce.2
  278.0 113.4 all-reduce.4
where the time goes:
time: 407 us; the launch traced here: 406 us
  waiting for transfers between devices  176 us (43%)
  other arithmetic  120 us (29%)
  matrix products  53.6 us (13%)
  local copies, waits for them, and re-layouts  23.1 us (6%)
  blocking collectives  18.9 us (5%)
  between operations  14.3 us (4%)
    psum x1, waiting for transfers between devices, local_step(): proj_sum = lax.psum(proj_part, 'tp')  113 us
    select_n x1, other arithmetic, local_step(): v_out = jnp.where(slot_hit, v_new[:, None], v_cache)  83.9 us
    psum x1, waiting for transfers between devices, local_step(): merged = lax.psum(packed, 'sp')  63.1 us
    pmax x1, blocking collectives, local_step(): global_max = lax.pmax(block_max, 'sp')  18.9 us
    dot_general x1, matrix products, local_step(): jnp.einsum('bgrt,btgd->bgrd', exp_w.astype(jnp.bfloat16), v_out, preferre...  16.3 us
    dot_general x1, matrix products, local_step(): jnp.einsum('bgrd,btgd->bgrt', q_rot, k_out, preferred_element_type=jnp.fl...  16.3 us
    reduce_sum x1, other arithmetic, local_step(): block_sum = jnp.sum(exp_w, axis=-1)  14.3 us
  transfers between devices with their start and end apart: 2, of which 2 were waited for; matrix products, arithmetic and copies ran while one was open for 0% of the time, Pallas kernels for 0%

commit v1 on v0

v1 whole, which is shorter than its diff:
```python
import functools

import jax
import jax.numpy as jnp
from jax import lax
from jax.experimental import pallas as pl
from jax.experimental.pallas import tpu as pltpu
from jax.sharding import PartitionSpec as P

SOFT_CAP = 50.0
ROPE_BASE = 10000.0
NORM_EPS = 1e-6
NEG_FILL = -1e30
F32 = jnp.float32
BF16 = jnp.bfloat16


def rms_scale(tensor, gain_w):
    mean_sq = jnp.mean(tensor * tensor, axis=-1, keepdims=True)
    return tensor * lax.rsqrt(mean_sq + NORM_EPS) * (1.0 + gain_w)


def stream_kernel(cfg, pos_s, x_hbm, gain, cos_t, sin_t, wq_hbm, wk_hbm, wv_hbm, kc, vc, k_out, v_out, o_ref, lse_ref,
                  x_v, a_v, wq_v, wk_v, wv_v, q_s, kn_s, vn_s, kbuf, vbuf, p_s,
                  w_sem, kin, vin, kout, vout):
    rows, seq, kv, hd, blk, nbuf, lag = cfg
    nblk = rows // blk
    groups = blk // 2
    base = lax.axis_index('sp') * seq

    def k_in(j, s):
        return pltpu.make_async_copy(kc.at[pl.ds(j * blk, blk)], kbuf.at[s], kin.at[s])

    def v_in(j, s):
        return pltpu.make_async_copy(vc.at[pl.ds(j * blk, blk)], vbuf.at[s], vin.at[s])

    def k_o(j, s):
        return pltpu.make_async_copy(kbuf.at[s], k_out.at[pl.ds(j * blk, blk)], kout.at[s])

    def v_o(j, s):
        return pltpu.make_async_copy(vbuf.at[s], v_out.at[pl.ds(j * blk, blk)], vout.at[s])

    loads = [pltpu.make_async_copy(x_hbm, x_v, w_sem.at[0]), pltpu.make_async_copy(wq_hbm, wq_v, w_sem.at[1]),
             pltpu.make_async_copy(wk_hbm, wk_v, w_sem.at[2]), pltpu.make_async_copy(wv_hbm, wv_v, w_sem.at[3])]
    for c in loads:
        c.start()
    for s in range(nbuf):
        k_in(s, s).start()
        v_in(s, s).start()

    loads[0].wait()
    step = 32

    @pl.loop(0, rows // step)
    def _(i):
        r = pl.ds(pl.multiple_of(i * step, step), step)
        a_v[r, :] = rms_scale(x_v[r, :].astype(F32), gain[...]).astype(BF16)

    half = hd // 2
    nq = wq_v.shape[1] // hd

    def rope_store(acc, dst, h, stride):
        lo, hi = acc[:, :half], acc[:, half:]
        c, s = cos_t[...], sin_t[...]
        r_lo = (lo * c - hi * s).astype(BF16).astype(F32)
        r_hi = (hi * c + lo * s).astype(BF16).astype(F32)
        idx = pl.ds(h, rows, stride=stride)
        dst[0, idx, :] = r_lo
        dst[1, idx, :] = r_hi

    loads[1].wait()
    for h in range(nq):
        acc = jnp.dot(a_v[...], wq_v[:, h * hd:(h + 1) * hd], preferred_element_type=F32)
        rope_store(acc, q_s, h, nq)
    loads[2].wait()
    for h in range(kv):
        acc = jnp.dot(a_v[...], wk_v[:, h * hd:(h + 1) * hd], preferred_element_type=F32)
        rope_store(acc, kn_s, h, kv)
    loads[3].wait()
    for h in range(kv):
        acc = jnp.dot(a_v[...], wv_v[:, h * hd:(h + 1) * hd], preferred_element_type=F32)
        acc = acc.astype(BF16).astype(F32)
        idx = pl.ds(h, rows, stride=kv)
        vn_s[0, idx, :] = acc[:, :half]
        vn_s[1, idx, :] = acc[:, half:]

    ng = nq * 2
    width = 2 * seq * kv
    ri = lax.broadcasted_iota(jnp.int32, (ng, width), 0)
    ci = lax.broadcasted_iota(jnp.int32, (ng, width), 1)
    first = ri < nq
    same = jnp.logical_and(ri // nq == ci // (seq * kv), (ri % nq) // (nq // kv) == ci % kv)
    t_id = jnp.where(same, (ci % (seq * kv)) // kv + base, 1 << 20)
    scale = hd ** -0.5 / SOFT_CAP

    @pl.loop(0, nblk)
    def _(j):
        slot = lax.rem(j, nbuf)

        @pl.when(jnp.logical_and(j >= lag, j + nbuf - lag < nblk))
        def _():
            s2 = lax.rem(j - lag, nbuf)
            k_o(j - lag, s2).wait()
            k_in(j - lag + nbuf, s2).start()
            v_o(j - lag, s2).wait()
            v_in(j - lag + nbuf, s2).start()

        k_in(j, slot).wait()
        v_in(j, slot).wait()
        for i in range(blk):
            b = j * blk + i
            t = pos_s[b] - base
            hit = jnp.logical_and(t >= 0, t < seq)
            tt = jnp.clip(t, 0, seq - 1)
            r = pl.ds(kv * b, kv)
            for buf, new in ((kbuf, kn_s), (vbuf, vn_s)):
                row = jnp.concatenate([new[0, r, :], new[1, r, :]], axis=-1)
                old = buf[slot, i, tt].astype(F32)
                buf[slot, i, tt] = jnp.where(hit, row, old).astype(BF16)

        parts = []
        for g in range(groups):
            r = pl.ds(pl.multiple_of((j * groups + g) * ng, ng), ng)
            qg = jnp.concatenate([q_s[0, r, :], q_s[1, r, :]], axis=-1).astype(BF16)
            km = kbuf[slot, 2 * g:2 * g + 2].reshape(width, hd)
            s = lax.dot_general(qg, km, (((1,), (1,)), ((), ())), preferred_element_type=F32)
            s = SOFT_CAP * jnp.tanh(s * scale)
            b = j * blk + 2 * g
            lim = jnp.where(first, pos_s[b], pos_s[b + 1])
            parts.append(jnp.where(t_id <= lim, s, NEG_FILL))
        sc = jnp.concatenate(parts, axis=0)
        m = jnp.max(sc, axis=-1, keepdims=True)
        e = jnp.where(sc > 0.5 * NEG_FILL, jnp.exp(sc - m), 0.0)
        l = jnp.sum(e, axis=-1, keepdims=True)
        some = l > 0.0
        inv = jnp.where(some, 1.0 / jnp.where(some, l, 1.0), 0.0)
        p_s[...] = e.astype(BF16)
        for g in range(groups):
            vm = vbuf[slot, 2 * g:2 * g + 2].reshape(width, hd)
            o = jnp.dot(p_s[g * ng:(g + 1) * ng, :], vm, preferred_element_type=F32)
            o_ref[pl.ds(pl.multiple_of((j * groups + g) * ng, ng), ng), :] = o * inv[g * ng:(g + 1) * ng, :]
        lse = jnp.where(some, m + jnp.log(jnp.where(some, l, 1.0)), NEG_FILL)
        lse_t = jnp.broadcast_to(lse, (groups * ng, 128)).T
        lse_ref[pl.ds(j, 1), :] = lse_t[0:1, :]
        k_o(j, slot).start()
        v_o(j, slot).start()

    for i in range(nbuf):
        j = nblk - nbuf + i
        k_o(j, j % nbuf).wait()
        v_o(j, j % nbuf).wait()


def solution(mesh):
    cache_spec = P('dp', 'sp', 'tp', None)

    def local_step(x_in, cur_pos, w_pre, w_q, w_k, w_v, w_o, w_post, k_cache, v_cache):
        rows, seq, kv, hd = k_cache.shape
        d_model = x_in.shape[1]
        nq = w_q.shape[1] // hd
        half = hd // 2
        blk, nbuf, lag = 32, 8, 3
        nblk = rows // blk
        inv_freq = ROPE_BASE ** (-2.0 * jnp.arange(half, dtype=F32) / hd)
        ang = cur_pos.astype(F32)[:, None] * inv_freq[None, :]
        cos_t, sin_t = jnp.cos(ang), jnp.sin(ang)
        vmem, hbm = pl.BlockSpec(memory_space=pltpu.VMEM), pl.BlockSpec(memory_space=pl.ANY)
        dma = pltpu.SemaphoreType.DMA
        cfg = (rows, seq, kv, hd, blk, nbuf, lag)
        k_out, v_out, o_part, lse = pl.pallas_call(
            functools.partial(stream_kernel, cfg),
            name='stream',
            out_shape=[jax.ShapeDtypeStruct(k_cache.shape, BF16), jax.ShapeDtypeStruct(v_cache.shape, BF16),
                       jax.ShapeDtypeStruct((rows * nq, hd), F32), jax.ShapeDtypeStruct((nblk, blk * nq), F32)],
            in_specs=[pl.BlockSpec(memory_space=pltpu.SMEM), hbm, vmem, vmem, vmem, hbm, hbm, hbm, hbm, hbm],
            out_specs=[hbm, hbm, vmem, vmem],
            scratch_shapes=[
                pltpu.VMEM((rows, d_model), BF16), pltpu.VMEM((rows, d_model), BF16),
                pltpu.VMEM(w_q.shape, BF16), pltpu.VMEM(w_k.shape, BF16), pltpu.VMEM(w_v.shape, BF16),
                pltpu.VMEM((2, rows * nq, half), F32), pltpu.VMEM((2, rows * kv, half), F32), pltpu.VMEM((2, rows * kv, half), F32),
                pltpu.VMEM((nbuf, blk, seq, kv, hd), BF16), pltpu.VMEM((nbuf, blk, seq, kv, hd), BF16),
                pltpu.VMEM((blk * nq, 2 * seq * kv), BF16),
                dma((4,)), dma((nbuf,)), dma((nbuf,)), dma((nbuf,)), dma((nbuf,))],
            compiler_params=pltpu.CompilerParams(vmem_limit_bytes=66_000_000),
            cost_estimate=pl.CostEstimate(flops=10 ** 10, bytes_accessed=150_000_000, transcendentals=0),
        )(cur_pos, x_in, w_pre[None, :], cos_t, sin_t, w_q, w_k, w_v, k_cache, v_cache)

        block_out = o_part.reshape(rows, nq, hd)
        lse = lse.reshape(rows, nq)
        top = lax.pmax(lse, 'sp')
        weight = jnp.exp(lse - top)
        packed = jnp.concatenate([block_out * weight[..., None], weight[..., None]], axis=-1)
        merged = lax.psum(packed, 'sp')
        attn_out = (merged[..., :hd] / merged[..., hd:]).reshape(rows, nq * hd)
        proj_part = jnp.dot(attn_out.astype(BF16), w_o, preferred_element_type=F32)
        proj_sum = lax.psum(proj_part, 'tp')
        x_out = (x_in.astype(F32) + rms_scale(proj_sum, w_post)).astype(BF16)
        return x_out, k_out, v_out

    return jax.shard_map(local_step, mesh=mesh,
                         in_specs=(P('dp', None), P('dp'), P(None), P(None, 'tp'), P(None, 'tp'), P(None, 'tp'), P('tp', None), P(None), cache_spec, cache_spec),
                         out_specs=(P('dp', None), cache_spec, cache_spec), check_vma=False)
```

time: 407 us -> 273 us (0.67)
  other arithmetic: 120 us -> 11.6 us
  Pallas kernels: 0 us -> 54.1 us
  matrix products: 53.6 us -> 6.67 us
  waiting for transfers between devices: 176 us -> 160 us
  local copies, waits for them, and re-layouts: 23.1 us -> 9.68 us
    select_n x1 -> x0, other arithmetic: 83.9 us -> none  [local_step(): v_out = jnp.where(slot_hit, v_new[:, None], v_cache)]
    pallas_call x0 -> x1, Pallas kernels: none -> 54.1 us  [local_step(): pl.pallas_call(functools.partial(stream_kernel, cfg), name='stream', out_...]
    dot_general x6 -> x1, matrix products: 53.6 us -> 6.67 us  [local_step(): proj_part = jnp.dot(attn_out.astype(BF16), w_o, preferred_element_type=F32)]
    psum x1, waiting for transfers between devices: 63.1 us -> 47.1 us  [local_step(): merged = lax.psum(packed, 'sp')]
    reduce_sum x1 -> x0, other arithmetic: 14.3 us -> none  [local_step(): block_sum = jnp.sum(exp_w, axis=-1)]
    div x1 -> x0, local copies, waits for them, and re-layouts: 6.76 us -> none  [local_step(): merged[..., :head_dim] / merged[..., head_dim:]]
    broadcast_in_dim x1 -> x2, local copies, waits for them, and re-layouts: 6.46 us -> 1.41 us  [the longest x1 1.31 us: local_step(): w_pre[None, :]]
where the time goes in v1:
time: 273 us
  waiting for transfers between devices  160 us (59%)
  Pallas kernels  54.1 us (20%)
  blocking collectives  16.5 us (6%)
  between operations  14.1 us (5%)
  other arithmetic  11.6 us (4%)
  local copies, waits for them, and re-layouts  9.68 us (4%)
  matrix products  6.67 us (2%)
    psum x1, waiting for transfers between devices, local_step(): proj_sum = lax.psum(proj_part, 'tp')  113 us
    pallas_call x1, Pallas kernels, local_step(): pl.pallas_call(functools.partial(stream_kernel, cfg), name='stream', out_...  54.1 us
    psum x1, waiting for transfers between devices, local_step(): merged = lax.psum(packed, 'sp')  47.1 us
    pmax x1, blocking collectives, local_step(): top = lax.pmax(lse, 'sp')  16.5 us
    dot_general x1, matrix products, local_step(): proj_part = jnp.dot(attn_out.astype(BF16), w_o, preferred_element_type=F32)  6.67 us
  transfers between devices with their start and end apart: 2, of which 2 were waited for; matrix products, arithmetic and copies ran while one was open for 0% of the time, Pallas kernels for 0%

profile of v1, /device:TPU:0, one launch (start us, length us, event | category | flops | bytes accessed | tf_op | source)
XLA Modules:
  0.0 272.8 jit_solution(572093376619183398)
XLA Ops:
  7.2 0.0 all-reduce.3.cloned.1.call-start
  7.2 0.7 convert_element_type.16
  7.9 1.3 broadcast_in_dim.4.gain
  9.2 1.8 multiply_sine_fusion
  11.0 54.1 %stream.1 = (bf16[512,64,2,256]{3,2,1,0:T(2,128)(2,1)}, bf16[512,64,2,256]{3,2,1,0:T(2,128)(2,1)}, f32[2048,256]{1,0:T(8,128)}, f32[16,128]{1,0:T(8,128)}) custom-call(s32[512]{0:T(512)} %pos_s.1, bf16[512,2304]{1,0:T(8,128)(2,1)} %x_hbm.1, f32[1,2304]{1,0:T(1,128)} %broadcast_in_dim.4.gain, f32[512,128]{1,0:T(8,128)} %get-tuple-element.12.cos_t, ...), custom_call_target="tpu_custom_call" | custom-call | flops 10000000000 | bytes 150000000 | tf_op jit(solution)/shard_map/stream/pallas_call | solution.py:170
  65.1 1.0 reshape.31
  66.1 16.5 %pmax.7 = f32[512,4]{1,0:T(8,128)S(1)} all-reduce(f32[512,4]{1,0:T(8,128)S(1)} %reshape.31), channel_id=1, replica_groups=mesh['dp'=1,'tp'=2,'sp'=4] {'sp'}, use_global_device_ids=true, to_apply=%region_0.0 | all-reduce | flops 2048 | bytes 16384 | tf_op jit(solution)/shard_map/pmax | solution.py:190
  82.7 0.1 copy.17
  82.8 2.9 %reshape.30 = f32[512,4,256]{2,1,0:T(4,128)} reshape(f32[2048,256]{1,0:T(8,128)} %get-tuple-element.7) | data formatting | bytes 4194304 | tf_op jit(solution)/shard_map/reshape | solution.py:188
  85.7 1.9 copy.18
  87.6 0.1 copy.19
  87.7 0.3 broadcast_multiply_fusion
  88.0 1.6 pad_maximum_fusion
  89.5 0.0 all-reduce.3.cloned.1.call-update
  89.5 0.0 all-reduce.5.cloned.1.call-start
  89.6 47.1 %all-reduce.3.cloned.1.call-done = f32[512,4,257]{0,2,1:T(8,128)} async-done(((f32[512,4,257]{0,2,1:T(8,128)}), f32[512,4,257]{0,2,1:T(8,128)}) %all-reduce.3.cloned.1.call-update) | async-done | bytes 2105360 | tf_op jit(solution)/shard_map/psum | solution.py:193
  136.7 0.8 slice.9
  137.6 1.9 fusion
  139.4 6.7 %fusion.1 = f32[512,2304]{1,0:T(8,128)} fusion(bf16[512,1024]{0,1:T(8,128)(2,1)S(1)} %bitcast.7, bf16[1024,2304]{1,0:T(8,128)(2,1)} %param.16), kind=kOutput, calls=%fused_computation.13 | convolution fusion | flops 2415919104 | bytes 10485760 | tf_op jit(solution)/shard_map/dot_general | solution.py:195
  146.1 0.0 copy-start.2
  146.1 0.0 copy-start.1
  146.1 0.0 all-reduce.5.cloned.1.call-update
  146.1 0.7 copy-done.2
  146.8 112.9 %all-reduce.5.cloned.1.call-done = f32[512,2304]{1,0:T(8,128)} async-done(((f32[512,2304]{1,0:T(8,128)}), f32[512,2304]{1,0:T(8,128)}) %all-reduce.5.cloned.1.call-update) | async-done | bytes 4718608 | tf_op jit(solution)/shard_map/psum | solution.py:196
  259.8 0.0 copy-start
  259.8 2.9 %multiply_reduce_fusion = f32[512]{0:T(512)S(1)} fusion(f32[512,2304]{1,0:T(8,128)} %all-reduce.5.cloned.1.call-done), kind=kLoop, calls=%fused_computation.1 | loop fusion | flops 2358784 | bytes 4720640 | tf_op jit(solution)/shard_map/reduce_sum | solution.py:19
  262.6 0.0 copy-done.1
  262.7 0.9 copy-done
  263.5 2.5 add_convert_fusion
  (5 shorter events, 0.1 us)
Async XLA Ops:
  7.2 129.5 %all-reduce.3.cloned.1.call-start = ((), (), s32[]{:S(2)}) async-start(), calls=%async_computation | async-start | bytes 4325376 | tf_op jit(solution)/shard_map/psum | solution.py:193
  89.5 170.2 %all-reduce.5.cloned.1.call-start = ((), (), s32[]{:S(2)}) async-start(), calls=%async_computation.1 | async-start | bytes 9437184 | tf_op jit(solution)/shard_map/psum | solution.py:196
  146.1 0.7 copy-start.2
  146.1 116.5 %copy-start.1 = (bf16[512,2304]{1,0:T(8,128)(2,1)S(1)}, bf16[512,2304]{1,0:T(8,128)(2,1)}, u32[]{:S(2)}) copy-start(bf16[512,2304]{1,0:T(8,128)(2,1)} %x_hbm.1) | copy-start | bytes 7077892
  259.8 3.8 %copy-start = (f32[512,2304]{1,0:T(8,128)S(1)}, f32[512,2304]{1,0:T(8,128)}, u32[]{:S(2)}) copy-start(f32[512,2304]{1,0:T(8,128)} %all-reduce.5.cloned.1.call-done) | copy-start | bytes 14155780
Sparse Core Ops, SparseCore 0:
  89.7 46.9 all-reduce.2
  146.3 113.4 all-reduce.4

commit v2 on v1

--- a/solution.py
+++ b/solution.py
@@ -149,6 +149,192 @@
         j = nblk - nbuf + i
         k_o(j, j % nbuf).wait()
         v_o(j, j % nbuf).wait()
+
+
+MESH_ID = pl.DeviceIdType.MESH
+
+
+def merge_weights(a, b):
+    top = jnp.maximum(a, b)
+    ea, eb = jnp.exp(a - top), jnp.exp(b - top)
+    tot = ea + eb
+    return ea / tot, eb / tot, top + jnp.log(tot)
+
+
+def columns(row):
+    return jnp.broadcast_to(row, (128, 128)).T
+
+
+def finish_kernel(cfg, o_hbm, lse_hbm, x_hbm, gain, wo_hbm, out_ref,
+                  o_ref, lse_ref, x_ref, wo_v, r1, r1l, k2, k2l, s2, s2l, r2, r2l, wt, tmp, su, ku, ru, gat,
+                  l_sem, s_d1, r_d1, s_dl, r_dl, s_x, r_x, s_xl, r_xl, s_y, r_y, s_ax, r_ax, s_ay, r_ay, s_f, r_f, s_d2, r_d2):
+    nc, nq, hd = cfg
+    dp, tp, sp = lax.axis_index('dp'), lax.axis_index('tp'), lax.axis_index('sp')
+    core, xx = lax.rem(sp, 2), sp // 2
+    partner = (dp, tp, xx * 2 + 1 - core)
+    x_nbr = (dp, tp, (1 - xx) * 2 + core)
+    y_nbr = (dp, 1 - tp, sp)
+
+    def rcopy(src, dst, ss, rs, dev):
+        return pltpu.make_async_remote_copy(src_ref=src, dst_ref=dst, send_sem=ss, recv_sem=rs, device_id=dev, device_id_type=MESH_ID)
+
+    lse_load = pltpu.make_async_copy(lse_hbm, lse_ref, l_sem.at[0])
+    o_load = pltpu.make_async_copy(o_hbm, o_ref, l_sem.at[1])
+    wo_load = pltpu.make_async_copy(wo_hbm, wo_v, l_sem.at[2])
+    x_load = pltpu.make_async_copy(x_hbm, x_ref, l_sem.at[3])
+    for c in (lse_load, o_load, wo_load, x_load):
+        c.start()
+    barrier = pltpu.get_barrier_semaphore()
+    for dev in (partner, x_nbr, y_nbr):
+        pl.semaphore_signal(barrier, inc=1, device_id=dev, device_id_type=MESH_ID)
+    pl.semaphore_wait(barrier, 3)
+
+    def d1(c):
+        other = 2 * c + 1 - core
+        return rcopy(o_hbm.at[pl.ds(other * 128, 128)], r1.at[c], s_d1.at[c], r_d1.at[c], partner)
+
+    dl = rcopy(lse_hbm, r1l, s_dl, r_dl, partner)
+
+    def xs(c):
+        return rcopy(s2.at[c], r2.at[c], s_x.at[c], r_x.at[c], x_nbr)
+
+    def xl(c):
+        return rcopy(s2l.at[c], r2l.at[c], s_xl.at[c], r_xl.at[c], x_nbr)
+
+    def ys(c):
+        return rcopy(su.at[c], ru.at[c], s_y.at[c], r_y.at[c], y_nbr)
+
+    def blk(c, x, y):
+        return c * 8 + core * 4 + x * 2 + y
+
+    def ag(c, sems, rsems, dev):
+        g = gat.at[blk(c, xx, tp)]
+        return rcopy(g, g, sems.at[c], rsems.at[c], dev)
+
+    def fw_y(c):
+        g = gat.at[blk(c, 1 - xx, tp)]
+        return rcopy(g, g, s_f.at[c], r_f.at[c], y_nbr)
+
+    def fw_x(c):
+        g = gat.at[blk(c, xx, 1 - tp)]
+        return rcopy(g, g, s_f.at[c], r_f.at[c], x_nbr)
+
+    def d2(c):
+        g = gat.at[pl.ds(c * 8 + core * 4, 4)]
+        return rcopy(g, g, s_d2.at[c], r_d2.at[c], partner)
+
+    dl.start()
+
+    @pl.loop(0, nc)
+    def _(c):
+        d1(c).start()
+
+    for c in (lse_load, o_load, wo_load, x_load):
+        c.wait()
+    dl.wait_recv()
+
+    def stage_a(c):
+        d1(c).wait_recv()
+        mine = 2 * c + core
+        wa, wb, lse = merge_weights(lse_ref[pl.ds(mine, 1), :], r1l[pl.ds(mine, 1), :])
+        wa, wb = columns(wa), columns(wb)
+        r = pl.ds(pl.multiple_of(mine * 128, 128), 128)
+        for i in range(hd // 128):
+            col = slice(i * 128, (i + 1) * 128)
+            tmp[i] = o_ref[r, col] * wa + r1[c, :, col] * wb
+            k2[c, i] = tmp[i, pl.ds(pl.multiple_of(xx * 64, 64), 64), :]
+            s2[c, i] = tmp[i, pl.ds(pl.multiple_of((1 - xx) * 64, 64), 64), :]
+        k2l[c] = lse
+        s2l[c] = lse
+        xs(c).start()
+        xl(c).start()
+
+    def stage_b(c):
+        xs(c).wait_recv()
+        xl(c).wait_recv()
+        wa, wb, _ = merge_weights(k2l[c], r2l[c])
+        wt[0] = columns(wa)
+        wt[1] = columns(wb)
+        r = pl.ds(pl.multiple_of(xx * 64, 64), 64)
+        wa, wb = wt[0, r, :], wt[1, r, :]
+        for i in range(hd // 128):
+            tmp[i, 0:64, :] = k2[c, i] * wa + r2[c, i] * wb
+        parts = [tmp[i, pl.ds(h, 16, stride=nq), :] for h in range(nq) for i in range(hd // 128)]
+        attn = jnp.concatenate(parts, axis=-1).astype(BF16)
+        d_model = wo_v.shape[1]
+        for n in range(d_model // 256):
+            col = slice(n * 256, (n + 1) * 256)
+            u = jnp.dot(attn, wo_v[:, col], preferred_element_type=F32)
+            ku[c, :, col] = jnp.where(tp == 0, u[:8], u[8:])
+            su[c, :, col] = jnp.where(tp == 0, u[8:], u[:8])
+        ys(c).start()
+
+    def stage_c(c):
+        ys(c).wait_recv()
+        u = ku[c] + ru[c]
+        x = x_ref[pl.ds(pl.multiple_of(c * 64 + core * 32 + xx * 16, 16), 16), :].astype(F32)
+        x = jnp.where(tp == 0, x[:8], x[8:])
+        gat[blk(c, xx, tp)] = x + rms_scale(u, gain[...])
+        ag(c, s_ax, r_ax, x_nbr).start()
+        ag(c, s_ay, r_ay, y_nbr).start()
+
+    def stage_d(c):
+        ag(c, s_ax, r_ax, x_nbr).wait_recv()
+        ag(c, s_ay, r_ay, y_nbr).wait_recv()
+
+        @pl.when(lax.rem(c, 2) == 0)
+        def _():
+            fw_x(c).start()
+
+        @pl.when(lax.rem(c, 2) == 1)
+        def _():
+            fw_y(c).start()
+
+    def stage_e(c):
+        @pl.when(lax.rem(c, 2) == 0)
+        def _():
+            fw_x(c).wait_recv()
+
+        @pl.when(lax.rem(c, 2) == 1)
+        def _():
+            fw_y(c).wait_recv()
+
+        d2(c).start()
+
+    def stage_f(c):
+        d2(c).wait_recv()
+        for i in range(4):
+            both = gat[pl.ds(c * 8 + 2 * i, 2)]
+            out_ref[pl.ds(pl.multiple_of(c * 64 + 16 * i, 16), 16), :] = both.reshape(16, both.shape[-1]).astype(BF16)
+
+    def at(t, lag, stage):
+        c = t - lag
+
+        @pl.when(jnp.logical_and(c >= 0, c < nc))
+        def _():
+            stage(c)
+
+    @pl.loop(0, nc + 5)
+    def _(t):
+        at(t, 0, stage_a)
+        at(t, 2, stage_c)
+        at(t, 3, stage_d)
+        at(t, 1, stage_b)
+        at(t, 4, stage_e)
+        at(t, 5, stage_f)
+
+    dl.wait_send()
+
+    @pl.loop(0, nc)
+    def _(c):
+        d1(c).wait_send()
+        xs(c).wait_send()
+        xl(c).wait_send()
+        ys(c).wait_send()
+        ag(c, s_ax, r_ax, x_nbr).wait_send()
+        ag(c, s_ay, r_ay, y_nbr).wait_send()
+        fw_x(c).wait_send()
+        d2(c).wait_send()
 
 
 def solution(mesh):
@@ -185,16 +371,25 @@
             cost_estimate=pl.CostEstimate(flops=10 ** 10, bytes_accessed=150_000_000, transcendentals=0),
         )(cur_pos, x_in, w_pre[None, :], cos_t, sin_t, w_q, w_k, w_v, k_cache, v_cache)
 
-        block_out = o_part.reshape(rows, nq, hd)
-        lse = lse.reshape(rows, nq)
-        top = lax.pmax(lse, 'sp')
-        weight = jnp.exp(lse - top)
-        packed = jnp.concatenate([block_out * weight[..., None], weight[..., None]], axis=-1)
-        merged = lax.psum(packed, 'sp')
-        attn_out = (merged[..., :hd] / merged[..., hd:]).reshape(rows, nq * hd)
-        proj_part = jnp.dot(attn_out.astype(BF16), w_o, preferred_element_type=F32)
-        proj_sum = lax.psum(proj_part, 'tp')
-        x_out = (x_in.astype(F32) + rms_scale(proj_sum, w_post)).astype(BF16)
+        nc, d_f32 = 8, (8, d_model)
+        x_out = pl.pallas_call(
+            functools.partial(finish_kernel, (nc, nq, hd)),
+            name='finish',
+            out_shape=jax.ShapeDtypeStruct(x_in.shape, BF16),
+            in_specs=[hbm, hbm, hbm, vmem, hbm],
+            out_specs=vmem,
+            scratch_shapes=[
+                pltpu.VMEM(o_part.shape, F32), pltpu.VMEM(lse.shape, F32), pltpu.VMEM(x_in.shape, BF16),
+                pltpu.VMEM(w_o.shape, BF16), pltpu.VMEM((nc, 128, hd), F32), pltpu.VMEM(lse.shape, F32),
+                pltpu.VMEM((nc, hd // 128, 64, 128), F32), pltpu.VMEM((nc, 1, 128), F32),
+                pltpu.VMEM((nc, hd // 128, 64, 128), F32), pltpu.VMEM((nc, 1, 128), F32),
+                pltpu.VMEM((nc, hd // 128, 64, 128), F32), pltpu.VMEM((nc, 1, 128), F32),
+                pltpu.VMEM((2, 128, 128), F32), pltpu.VMEM((hd // 128, 128, 128), F32),
+                pltpu.VMEM((nc,) + d_f32, F32), pltpu.VMEM((nc,) + d_f32, F32), pltpu.VMEM((nc,) + d_f32, F32),
+                pltpu.VMEM((8 * nc,) + d_f32, F32),
+                dma((4,)), dma((nc,)), dma((nc,)), dma, dma] + [dma((nc,))] * 14,
+            compiler_params=pltpu.CompilerParams(vmem_limit_bytes=66_000_000, collective_id=0, has_side_effects=True),
+        )(o_part, lse, x_in, w_post[None, :], w_o)
         return x_out, k_out, v_out
 
     return jax.shard_map(local_step, mesh=mesh,

time: 273 us -> 129 us (0.47)
  waiting for transfers between devices: 160 us -> 0 us
  Pallas kernels: 54.1 us -> 119 us
  blocking collectives: 16.5 us -> 0 us
  between operations: 14.1 us -> 0.65 us
  other arithmetic: 11.6 us -> 2.49 us
  matrix products: 6.67 us -> 0 us
  local copies, waits for them, and re-layouts: 9.68 us -> 5.84 us
    psum x2 -> x0, waiting for transfers between devices: 160 us -> none  [the longest x1 113 us: local_step(): proj_sum = lax.psum(proj_part, 'tp')]
    pallas_call x0 -> x1, Pallas kernels: none -> 65.2 us  [local_step(): pl.pallas_call(functools.partial(finish_kernel, (nc, nq, hd)), name='fini...]
    pmax x1 -> x0, blocking collectives: 16.5 us -> none  [local_step(): top = lax.pmax(lse, 'sp')]
    dot_general x1 -> x0, matrix products: 6.67 us -> none  [local_step(): proj_part = jnp.dot(attn_out.astype(BF16), w_o, preferred_element_type=F32)]
    reshape x3 -> x0, local copies, waits for them, and re-layouts: 5.77 us -> none  [the longest x2 4.81 us: local_step(): block_out = o_part.reshape(rows, nq, hd)]
    convert_element_type x2 -> x0, other arithmetic: 4.33 us -> none  [the longest x1 2.46 us: local_step(): x_out = (x_in.astype(F32) + rms_scale(proj_sum, w_post)).astype(BF16)]
    reduce_sum x1 -> x0, other arithmetic: 2.87 us -> none  [rms_scale(): mean_sq = jnp.mean(tensor * tensor, axis=-1, keepdims=True)]
  transfers between devices with their start and end apart: 2 -> 0, of which waited for: 2 -> 0; matrix products, arithmetic and copies ran while one was open for 0% -> 0% of each run, Pallas kernels for 0% -> 0%
where the time goes in v2:
time: 129 us; the launch traced here: 128 us
  Pallas kernels  119 us (92%)
  local copies, waits for them, and re-layouts  5.84 us (5%)
  other arithmetic  2.49 us (2%)
    pallas_call x1, Pallas kernels, local_step(): pl.pallas_call(functools.partial(finish_kernel, (nc, nq, hd)), name='fini...  65.2 us
    pallas_call x1, Pallas kernels, local_step(): pl.pallas_call(functools.partial(stream_kernel, cfg), name='stream', out_...  54.1 us
    unnamed x1, local copies, waits for them, and re-layouts  3.22 us

profile of v2, /device:TPU:0, one launch (start us, length us, event | category | flops | bytes accessed | tf_op | source)
XLA Modules:
  0.0 128.3 jit_solution(659270228547883258)
XLA Ops:
  0.6 0.7 convert_element_type.3
  1.3 1.3 %broadcast_in_dim.8.gain = f32[1,2304]{1,0:T(1,128)} reshape(f32[2304]{0:T(1024)} %param.12) | data formatting | bytes 18432 | tf_op jit(solution)/shard_map/broadcast_in_dim | solution.py:372
  2.6 1.3 %broadcast_in_dim.9.gain = f32[1,2304]{1,0:T(1,128)} reshape(f32[2304]{0:T(1024)} %param.17) | data formatting | bytes 18432 | tf_op jit(solution)/shard_map/broadcast_in_dim | solution.py:392
  3.9 1.8 %multiply_sine_fusion = (f32[512,128]{1,0:T(8,128)}, f32[512,128]{1,0:T(8,128)}) fusion(f32[128]{0:T(128)S(1)} %multiply_power_fusion, f32[512]{0:T(512)S(1)} %convert_element_type.3), kind=kLoop, calls=%fused_computation | loop fusion | flops 65536 | bytes 526848 | tf_op jit(solution)/shard_map/sin | solution.py:352
  5.7 54.1 %stream.1 = (bf16[512,64,2,256]{3,2,1,0:T(2,128)(2,1)}, bf16[512,64,2,256]{3,2,1,0:T(2,128)(2,1)}, f32[2048,256]{1,0:T(8,128)}, f32[16,128]{1,0:T(8,128)}) custom-call(s32[512]{0:T(512)} %pos_s.1, bf16[512,2304]{1,0:T(8,128)(2,1)} %x_hbm.3, f32[1,2304]{1,0:T(1,128)} %broadcast_in_dim.8.gain, f32[512,128]{1,0:T(8,128)} %get-tuple-element.12.cos_t, ...), custom_call_target="tpu_custom_call" | custom-call | flops 10000000000 | bytes 150000000 | tf_op jit(solution)/shard_map/stream/pallas_call | solution.py:356
  59.9 65.2 %finish.1 = bf16[512,2304]{1,0:T(8,128)(2,1)} custom-call(f32[2048,256]{1,0:T(8,128)} %get-tuple-element.7.o_hbm, f32[16,128]{1,0:T(8,128)} %get-tuple-element.8.lse_hbm, bf16[512,2304]{1,0:T(8,128)(2,1)} %x_hbm.3, f32[1,2304]{1,0:T(1,128)} %broadcast_in_dim.9.gain, bf16[1024,2304]{1,0:T(8,128)(2,1)} %wo_hbm.1), custom_call_target="tpu_custom_call" | custom-call | tf_op jit(solution)/shard_map/finish/pallas_call | solution.py:375
  125.1 3.2 %copy.14 = bf16[512,2304]{1,0:T(8,128)(2,1)} copy(bf16[512,2304]{1,0:T(8,128)(2,1)} %finish.1) | data formatting | bytes 4718592
  (1 shorter events, 0.0 us)

commit v3 on v2

--- a/solution.py
+++ b/solution.py
@@ -2,6 +2,7 @@
 
 import jax
 import jax.numpy as jnp
+import numpy as np
 from jax import lax
 from jax.experimental import pallas as pl
 from jax.experimental.pallas import tpu as pltpu
@@ -20,12 +21,13 @@
     return tensor * lax.rsqrt(mean_sq + NORM_EPS) * (1.0 + gain_w)
 
 
-def stream_kernel(cfg, pos_s, x_hbm, gain, cos_t, sin_t, wq_hbm, wk_hbm, wv_hbm, kc, vc, k_out, v_out, o_ref, lse_ref,
-                  x_v, a_v, wq_v, wk_v, wv_v, q_s, kn_s, vn_s, kbuf, vbuf, p_s,
+def stream_kernel(cfg, pos_s, pos_v, freq, x_hbm, gain, wq_hbm, wk_hbm, wv_hbm, kc, vc, k_out, v_out, o_ref, lse_ref,
+                  a_v, wq_v, wk_v, wv_v, cs, q_s, kn_s, vn_s, kbuf, vbuf, p_s,
                   w_sem, kin, vin, kout, vout):
     rows, seq, kv, hd, blk, nbuf, lag = cfg
     nblk = rows // blk
     groups = blk // 2
+    half = hd // 2
     base = lax.axis_index('sp') * seq
 
     def k_in(j, s):
@@ -40,28 +42,33 @@
     def v_o(j, s):
         return pltpu.make_async_copy(vbuf.at[s], v_out.at[pl.ds(j * blk, blk)], vout.at[s])
 
-    loads = [pltpu.make_async_copy(x_hbm, x_v, w_sem.at[0]), pltpu.make_async_copy(wq_hbm, wq_v, w_sem.at[1]),
+    loads = [pltpu.make_async_copy(x_hbm, a_v, w_sem.at[0]), pltpu.make_async_copy(wq_hbm, wq_v, w_sem.at[1]),
              pltpu.make_async_copy(wk_hbm, wk_v, w_sem.at[2]), pltpu.make_async_copy(wv_hbm, wv_v, w_sem.at[3])]
     for c in loads:
         c.start()
+
+    for i in range(rows // 128):
+        ang = jnp.broadcast_to(pos_v[i:i + 1, :].astype(F32), (128, 128)).T * freq[...]
+        cs[0, i * 128:(i + 1) * 128, :] = jnp.cos(ang)
+        cs[1, i * 128:(i + 1) * 128, :] = jnp.sin(ang)
+
+    loads[0].wait()
+    step = 32
+
+    @pl.loop(0, rows // step)
+    def _(i):
+        r = pl.ds(pl.multiple_of(i * step, step), step)
+        a_v[r, :] = rms_scale(a_v[r, :].astype(F32), gain[...]).astype(BF16)
+
     for s in range(nbuf):
         k_in(s, s).start()
         v_in(s, s).start()
 
-    loads[0].wait()
-    step = 32
-
-    @pl.loop(0, rows // step)
-    def _(i):
-        r = pl.ds(pl.multiple_of(i * step, step), step)
-        a_v[r, :] = rms_scale(x_v[r, :].astype(F32), gain[...]).astype(BF16)
-
-    half = hd // 2
     nq = wq_v.shape[1] // hd
 
     def rope_store(acc, dst, h, stride):
         lo, hi = acc[:, :half], acc[:, half:]
-        c, s = cos_t[...], sin_t[...]
+        c, s = cs[0], cs[1]
         r_lo = (lo * c - hi * s).astype(BF16).astype(F32)
         r_hi = (hi * c + lo * s).astype(BF16).astype(F32)
         idx = pl.ds(h, rows, stride=stride)
@@ -113,10 +120,10 @@
             hit = jnp.logical_and(t >= 0, t < seq)
             tt = jnp.clip(t, 0, seq - 1)
             r = pl.ds(kv * b, kv)
-            for buf, new in ((kbuf, kn_s), (vbuf, vn_s)):
-                row = jnp.concatenate([new[0, r, :], new[1, r, :]], axis=-1)
-                old = buf[slot, i, tt].astype(F32)
-                buf[slot, i, tt] = jnp.where(hit, row, old).astype(BF16)
+            row = jnp.concatenate([kn_s[0, r, :], kn_s[1, r, :]], axis=-1)
+            kbuf[slot, i, tt] = jnp.where(hit, row, kbuf[slot, i, tt].astype(F32)).astype(BF16)
+            row = jnp.concatenate([vn_s[0, r, :], vn_s[1, r, :]], axis=-1)
+            vbuf[slot, i, tt] = jnp.where(hit, row, vbuf[slot, i, tt].astype(F32)).astype(BF16)
 
         parts = []
         for g in range(groups):
@@ -165,8 +172,8 @@
     return jnp.broadcast_to(row, (128, 128)).T
 
 
-def finish_kernel(cfg, o_hbm, lse_hbm, x_hbm, gain, wo_hbm, out_ref,
-                  o_ref, lse_ref, x_ref, wo_v, r1, r1l, k2, k2l, s2, s2l, r2, r2l, wt, tmp, su, ku, ru, gat,
+def finish_kernel(cfg, o_ref, lse_ref, x_hbm, gain, wo_hbm, out_ref,
+                  x_ref, wo_v, r1, r1l, k2, k2l, s2, s2l, r2, r2l, wt, tmp, su, ku, ru, gat,
                   l_sem, s_d1, r_d1, s_dl, r_dl, s_x, r_x, s_xl, r_xl, s_y, r_y, s_ax, r_ax, s_ay, r_ay, s_f, r_f, s_d2, r_d2):
     nc, nq, hd = cfg
     dp, tp, sp = lax.axis_index('dp'), lax.axis_index('tp'), lax.axis_index('sp')
@@ -178,12 +185,10 @@
     def rcopy(src, dst, ss, rs, dev):
         return pltpu.make_async_remote_copy(src_ref=src, dst_ref=dst, send_sem=ss, recv_sem=rs, device_id=dev, device_id_type=MESH_ID)
 
-    lse_load = pltpu.make_async_copy(lse_hbm, lse_ref, l_sem.at[0])
-    o_load = pltpu.make_async_copy(o_hbm, o_ref, l_sem.at[1])
-    wo_load = pltpu.make_async_copy(wo_hbm, wo_v, l_sem.at[2])
-    x_load = pltpu.make_async_copy(x_hbm, x_ref, l_sem.at[3])
-    for c in (lse_load, o_load, wo_load, x_load):
-        c.start()
+    wo_load = pltpu.make_async_copy(wo_hbm, wo_v, l_sem.at[0])
+    x_load = pltpu.make_async_copy(x_hbm, x_ref, l_sem.at[1])
+    wo_load.start()
+    x_load.start()
     barrier = pltpu.get_barrier_semaphore()
     for dev in (partner, x_nbr, y_nbr):
         pl.semaphore_signal(barrier, inc=1, device_id=dev, device_id_type=MESH_ID)
@@ -191,9 +196,9 @@
 
     def d1(c):
         other = 2 * c + 1 - core
-        return rcopy(o_hbm.at[pl.ds(other * 128, 128)], r1.at[c], s_d1.at[c], r_d1.at[c], partner)
-
-    dl = rcopy(lse_hbm, r1l, s_dl, r_dl, partner)
+        return rcopy(o_ref.at[pl.ds(other * 128, 128)], r1.at[c], s_d1.at[c], r_d1.at[c], partner)
+
+    dl = rcopy(lse_ref, r1l, s_dl, r_dl, partner)
 
     def xs(c):
         return rcopy(s2.at[c], r2.at[c], s_x.at[c], r_x.at[c], x_nbr)
@@ -229,8 +234,6 @@
     def _(c):
         d1(c).start()
 
-    for c in (lse_load, o_load, wo_load, x_load):
-        c.wait()
     dl.wait_recv()
 
     def stage_a(c):
@@ -282,20 +285,20 @@
         ag(c, s_ax, r_ax, x_nbr).wait_recv()
         ag(c, s_ay, r_ay, y_nbr).wait_recv()
 
-        @pl.when(lax.rem(c, 2) == 0)
+        @pl.when(lax.rem(c, 3) != 2)
         def _():
             fw_x(c).start()
 
-        @pl.when(lax.rem(c, 2) == 1)
+        @pl.when(lax.rem(c, 3) == 2)
         def _():
             fw_y(c).start()
 
     def stage_e(c):
-        @pl.when(lax.rem(c, 2) == 0)
+        @pl.when(lax.rem(c, 3) != 2)
         def _():
             fw_x(c).wait_recv()
 
-        @pl.when(lax.rem(c, 2) == 1)
+        @pl.when(lax.rem(c, 3) == 2)
         def _():
             fw_y(c).wait_recv()
 
@@ -314,14 +317,20 @@
         def _():
             stage(c)
 
-    @pl.loop(0, nc + 5)
+    @pl.loop(0, nc + 9)
     def _(t):
         at(t, 0, stage_a)
-        at(t, 2, stage_c)
-        at(t, 3, stage_d)
-        at(t, 1, stage_b)
-        at(t, 4, stage_e)
-        at(t, 5, stage_f)
+
+        @pl.when(t == 2)
+        def _():
+            wo_load.wait()
+            x_load.wait()
+
+        at(t, 2, stage_b)
+        at(t, 4, stage_c)
+        at(t, 6, stage_d)
+        at(t, 8, stage_e)
+        at(t, 9, stage_f)
 
     dl.wait_send()
 
@@ -347,9 +356,7 @@
         half = hd // 2
         blk, nbuf, lag = 32, 8, 3
         nblk = rows // blk
-        inv_freq = ROPE_BASE ** (-2.0 * jnp.arange(half, dtype=F32) / hd)
-        ang = cur_pos.astype(F32)[:, None] * inv_freq[None, :]
-        cos_t, sin_t = jnp.cos(ang), jnp.sin(ang)
+        inv_freq = (ROPE_BASE ** (-2.0 * np.arange(half) / hd)).astype(np.float32)[None, :]
         vmem, hbm = pl.BlockSpec(memory_space=pltpu.VMEM), pl.BlockSpec(memory_space=pl.ANY)
         dma = pltpu.SemaphoreType.DMA
         cfg = (rows, seq, kv, hd, blk, nbuf, lag)
@@ -357,29 +364,30 @@
             functools.partial(stream_kernel, cfg),
             name='stream',
             out_shape=[jax.ShapeDtypeStruct(k_cache.shape, BF16), jax.ShapeDtypeStruct(v_cache.shape, BF16),
-                       jax.ShapeDtypeStruct((rows * nq, hd), F32), jax.ShapeDtypeStruct((nblk, blk * nq), F32)],
-            in_specs=[pl.BlockSpec(memory_space=pltpu.SMEM), hbm, vmem, vmem, vmem, hbm, hbm, hbm, hbm, hbm],
+                       pltpu.VMEM((rows * nq, hd), F32), pltpu.VMEM((nblk, blk * nq), F32)],
+            in_specs=[pl.BlockSpec(memory_space=pltpu.SMEM), vmem, vmem, hbm, vmem, hbm, hbm, hbm, hbm, hbm],
             out_specs=[hbm, hbm, vmem, vmem],
             scratch_shapes=[
-                pltpu.VMEM((rows, d_model), BF16), pltpu.VMEM((rows, d_model), BF16),
+                pltpu.VMEM((rows, d_model), BF16),
                 pltpu.VMEM(w_q.shape, BF16), pltpu.VMEM(w_k.shape, BF16), pltpu.VMEM(w_v.shape, BF16),
+                pltpu.VMEM((2, rows, half), F32),
                 pltpu.VMEM((2, rows * nq, half), F32), pltpu.VMEM((2, rows * kv, half), F32), pltpu.VMEM((2, rows * kv, half), F32),
                 pltpu.VMEM((nbuf, blk, seq, kv, hd), BF16), pltpu.VMEM((nbuf, blk, seq, kv, hd), BF16),
                 pltpu.VMEM((blk * nq, 2 * seq * kv), BF16),
                 dma((4,)), dma((nbuf,)), dma((nbuf,)), dma((nbuf,)), dma((nbuf,))],
-            compiler_params=pltpu.CompilerParams(vmem_limit_bytes=66_000_000),
+            compiler_params=pltpu.CompilerParams(vmem_limit_bytes=57_000_000),
             cost_estimate=pl.CostEstimate(flops=10 ** 10, bytes_accessed=150_000_000, transcendentals=0),
-        )(cur_pos, x_in, w_pre[None, :], cos_t, sin_t, w_q, w_k, w_v, k_cache, v_cache)
+        )(cur_pos, cur_pos.reshape(rows // 128, 128), inv_freq, x_in, w_pre, w_q, w_k, w_v, k_cache, v_cache)
 
         nc, d_f32 = 8, (8, d_model)
         x_out = pl.pallas_call(
             functools.partial(finish_kernel, (nc, nq, hd)),
             name='finish',
-            out_shape=jax.ShapeDtypeStruct(x_in.shape, BF16),
-            in_specs=[hbm, hbm, hbm, vmem, hbm],
+            out_shape=pltpu.VMEM(x_in.shape, BF16),
+            in_specs=[vmem, vmem, hbm, vmem, hbm],
             out_specs=vmem,
             scratch_shapes=[
-                pltpu.VMEM(o_part.shape, F32), pltpu.VMEM(lse.shape, F32), pltpu.VMEM(x_in.shape, BF16),
+                pltpu.VMEM(x_in.shape, BF16),
                 pltpu.VMEM(w_o.shape, BF16), pltpu.VMEM((nc, 128, hd), F32), pltpu.VMEM(lse.shape, F32),
                 pltpu.VMEM((nc, hd // 128, 64, 128), F32), pltpu.VMEM((nc, 1, 128), F32),
                 pltpu.VMEM((nc, hd // 128, 64, 128), F32), pltpu.VMEM((nc, 1, 128), F32),
@@ -387,9 +395,10 @@
                 pltpu.VMEM((2, 128, 128), F32), pltpu.VMEM((hd // 128, 128, 128), F32),
                 pltpu.VMEM((nc,) + d_f32, F32), pltpu.VMEM((nc,) + d_f32, F32), pltpu.VMEM((nc,) + d_f32, F32),
                 pltpu.VMEM((8 * nc,) + d_f32, F32),
-                dma((4,)), dma((nc,)), dma((nc,)), dma, dma] + [dma((nc,))] * 14,
-            compiler_params=pltpu.CompilerParams(vmem_limit_bytes=66_000_000, collective_id=0, has_side_effects=True),
-        )(o_part, lse, x_in, w_post[None, :], w_o)
+                dma((2,)), dma((nc,)), dma((nc,)), dma, dma] + [dma((nc,))] * 14,
+            compiler_params=pltpu.CompilerParams(vmem_limit_bytes=50_000_000, collective_id=0, has_side_effects=True),
+            cost_estimate=pl.CostEstimate(flops=10 ** 10, bytes_accessed=100_000_000, transcendentals=0),
+        )(o_part, lse, x_in, w_post, w_o)
         return x_out, k_out, v_out
 
     return jax.shard_map(local_step, mesh=mesh,

time: 129 us -> 95.3 us (0.74)
  Pallas kernels: 119 us -> 93.1 us
  local copies, waits for them, and re-layouts: 5.84 us -> 1.41 us
  other arithmetic: 2.49 us -> 0 us
    pallas_call x1, Pallas kernels: 65.2 us -> 44.3 us  [local_step(): pl.pallas_call(functools.partial(finish_kernel, (nc, nq, hd)), name='fini...]
    pallas_call x1, Pallas kernels: 54.1 us -> 48.8 us  [local_step(): pl.pallas_call(functools.partial(stream_kernel, cfg), name='stream', out_...]
    broadcast_in_dim x2 -> x0, local copies, waits for them, and re-layouts: 2.62 us -> none  [the longest x1 1.31 us: local_step(): w_post[None, :]]
    unnamed x1 -> x3, local copies, waits for them, and re-layouts: 3.22 us -> 1.41 us
    sin x1 -> x0, other arithmetic: 1.79 us -> none  [local_step(): cos_t, sin_t = (jnp.cos(ang), jnp.sin(ang))]
where the time goes in v3:
time: 95.3 us; the launch traced here: 95.2 us
  Pallas kernels  93.1 us (98%)
  local copies, waits for them, and re-layouts  1.41 us (1%)
    pallas_call x1, Pallas kernels, local_step(): pl.pallas_call(functools.partial(stream_kernel, cfg), name='stream', out_...  48.8 us
    pallas_call x1, Pallas kernels, local_step(): pl.pallas_call(functools.partial(finish_kernel, (nc, nq, hd)), name='fini...  44.3 us

profile of v3, /device:TPU:0, one launch (start us, length us, event | category | flops | bytes accessed | tf_op | source)
XLA Modules:
  0.0 95.2 jit_solution(7398438215612383494)
XLA Ops:
  0.6 0.0 copy-start
  0.6 48.8 %stream.1 = (bf16[512,64,2,256]{3,2,1,0:T(2,128)(2,1)}, bf16[512,64,2,256]{3,2,1,0:T(2,128)(2,1)}, f32[2048,256]{1,0:T(8,128)S(1)}, f32[16,128]{1,0:T(8,128)S(1)}) custom-call(s32[512]{0:T(512)} %pos_s.1, s32[4,128]{1,0:T(4,128)} %bitcast.1, f32[1,128]{1,0:T(1,128)} %constant.2.clone.freq, bf16[512,2304]{1,0:T(8,128)(2,1)} %x_hbm.3, f32[2304]{0:T(1024)} %gain.2, ...), custom_call_target="tpu_custom_call" | custom-call | flops 10000000000 | bytes 150000000 | tf_op jit(solution)/shard_map/stream/pallas_call | solution.py:363
  49.5 0.0 copy-done
  49.5 44.3 %finish.1 = bf16[512,2304]{1,0:T(8,128)(2,1)S(1)} custom-call(f32[2048,256]{1,0:T(8,128)S(1)} %get-tuple-element.7.o_ref, f32[16,128]{1,0:T(8,128)S(1)} %get-tuple-element.8.lse_ref, bf16[512,2304]{1,0:T(8,128)(2,1)} %x_hbm.3, f32[2304]{0:T(1024)S(1)} %copy-done, bf16[1024,2304]{1,0:T(8,128)(2,1)} %wo_hbm.1), custom_call_target="tpu_custom_call" | custom-call | flops 10000000000 | bytes 100000000 | tf_op jit(solution)/shard_map/finish/pallas_call | solution.py:383
  93.8 1.4 %copy.15 = bf16[512,2304]{1,0:T(8,128)(2,1)} copy(bf16[512,2304]{1,0:T(8,128)(2,1)S(1)} %finish.1) | data formatting | bytes 4718592
Async XLA Ops:
  0.6 48.9 %copy-start = (f32[2304]{0:T(1024)S(1)}, f32[2304]{0:T(1024)}, u32[]{:S(2)}) copy-start(f32[2304]{0:T(1024)} %gain.3) | copy-start | bytes 27652

commit v4 on v3

--- a/solution.py
+++ b/solution.py
@@ -21,11 +21,57 @@
     return tensor * lax.rsqrt(mean_sq + NORM_EPS) * (1.0 + gain_w)
 
 
-def stream_kernel(cfg, pos_s, pos_v, freq, x_hbm, gain, wq_hbm, wk_hbm, wv_hbm, kc, vc, k_out, v_out, o_ref, lse_ref,
+def score_ids(nq, seq, kv, base):
+    ng, width = nq * 2, 2 * seq * kv
+    ri = lax.broadcasted_iota(jnp.int32, (ng, width), 0)
+    ci = lax.broadcasted_iota(jnp.int32, (ng, width), 1)
+    same = jnp.logical_and(ri // nq == ci // (seq * kv), (ri % nq) // (nq // kv) == ci % kv)
+    return ng, width, ri < nq, jnp.where(same, (ci % (seq * kv)) // kv + base, 1 << 20)
+
+
+def attend(k_of, v_of, q_of, lim_of, put, groups, ng, t_id, p_s, new=None):
+    scale = k_of(0).shape[1] ** -0.5 / SOFT_CAP
+    parts, hits = [], []
+    if new is not None:
+        q_lo, q_hi, k_lo, k_hi, v_lo, v_hi = new
+        s_new = SOFT_CAP * jnp.tanh(jnp.sum(q_lo * k_lo + q_hi * k_hi, axis=-1, keepdims=True) * scale)
+    for g in range(groups):
+        s = lax.dot_general(q_of(g).astype(BF16), k_of(g), (((1,), (1,)), ((), ())), preferred_element_type=F32)
+        s = SOFT_CAP * jnp.tanh(s * scale)
+        lim = lim_of(g)
+        if new is not None:
+            hit = t_id == lim
+            s = jnp.where(hit, s_new[g * ng:(g + 1) * ng, :], s)
+            hits.append(jnp.where(hit, 1.0, 0.0))
+        parts.append(jnp.where(t_id <= lim, s, NEG_FILL))
+    sc = jnp.concatenate(parts, axis=0)
+    m = jnp.max(sc, axis=-1, keepdims=True)
+    e = jnp.where(sc > 0.5 * NEG_FILL, jnp.exp(sc - m), 0.0)
+    l = jnp.sum(e, axis=-1, keepdims=True)
+    some = l > 0.0
+    inv = jnp.where(some, 1.0 / jnp.where(some, l, 1.0), 0.0)
+    if new is not None:
+        hit = jnp.concatenate(hits, axis=0)
+        e_new = jnp.sum(e * hit, axis=-1, keepdims=True)
+        e = e * (1.0 - hit)
+        own = jnp.concatenate([v_lo * e_new, v_hi * e_new], axis=-1)
+    p_s[...] = e.astype(BF16)
+    for g in range(groups):
+        r = slice(g * ng, (g + 1) * ng)
+        o = jnp.dot(p_s[r, :], v_of(g), preferred_element_type=F32)
+        if new is not None:
+            o = o + own[r, :]
+        put(g, o * inv[r, :])
+    lse = jnp.where(some, m + jnp.log(jnp.where(some, l, 1.0)), NEG_FILL)
+    return jnp.broadcast_to(lse, (groups * ng, 128)).T[0:1, :]
+
+
+def stream_kernel(cfg, pos_s, pos_v, freq, x_hbm, gain, wq_hbm, wk_hbm, wv_hbm, kc, vc, k_out, v_out, o_ref, lse_ref, q_c, ke_c, ve_c,
                   a_v, wq_v, wk_v, wv_v, cs, q_s, kn_s, vn_s, kbuf, vbuf, p_s,
                   w_sem, kin, vin, kout, vout):
-    rows, seq, kv, hd, blk, nbuf, lag = cfg
-    nblk = rows // blk
+    rows, early, seq, kv, hd, blk, nbuf, lag = cfg
+    late = rows - early
+    nblk = early // blk
     groups = blk // 2
     half = hd // 2
     base = lax.axis_index('sp') * seq
@@ -66,39 +112,32 @@
 
     nq = wq_v.shape[1] // hd
 
-    def rope_store(acc, dst, h, stride):
+    def spread(pair, dst, h, stride, dst_c, heads):
+        for i, part in enumerate(pair):
+            part = part.astype(BF16).astype(F32)
+            dst[i, pl.ds(h, early, stride=stride), :] = part[:early]
+            for hc in heads:
+                dst_c[i, pl.ds(hc, late, stride=nq), :] = part[early:]
+
+    def rope(acc):
         lo, hi = acc[:, :half], acc[:, half:]
-        c, s = cs[0], cs[1]
-        r_lo = (lo * c - hi * s).astype(BF16).astype(F32)
-        r_hi = (hi * c + lo * s).astype(BF16).astype(F32)
-        idx = pl.ds(h, rows, stride=stride)
-        dst[0, idx, :] = r_lo
-        dst[1, idx, :] = r_hi
-
+        return lo * cs[0] - hi * cs[1], hi * cs[0] + lo * cs[1]
+
+    share = nq // kv
     loads[1].wait()
     for h in range(nq):
         acc = jnp.dot(a_v[...], wq_v[:, h * hd:(h + 1) * hd], preferred_element_type=F32)
-        rope_store(acc, q_s, h, nq)
+        spread(rope(acc), q_s, h, nq, q_c, (h,))
     loads[2].wait()
     for h in range(kv):
         acc = jnp.dot(a_v[...], wk_v[:, h * hd:(h + 1) * hd], preferred_element_type=F32)
-        rope_store(acc, kn_s, h, kv)
+        spread(rope(acc), kn_s, h, kv, ke_c, range(h * share, (h + 1) * share))
     loads[3].wait()
     for h in range(kv):
         acc = jnp.dot(a_v[...], wv_v[:, h * hd:(h + 1) * hd], preferred_element_type=F32)
-        acc = acc.astype(BF16).astype(F32)
-        idx = pl.ds(h, rows, stride=kv)
-        vn_s[0, idx, :] = acc[:, :half]
-        vn_s[1, idx, :] = acc[:, half:]
-
-    ng = nq * 2
-    width = 2 * seq * kv
-    ri = lax.broadcasted_iota(jnp.int32, (ng, width), 0)
-    ci = lax.broadcasted_iota(jnp.int32, (ng, width), 1)
-    first = ri < nq
-    same = jnp.logical_and(ri // nq == ci // (seq * kv), (ri % nq) // (nq // kv) == ci % kv)
-    t_id = jnp.where(same, (ci % (seq * kv)) // kv + base, 1 << 20)
-    scale = hd ** -0.5 / SOFT_CAP
+        spread((acc[:, :half], acc[:, half:]), vn_s, h, kv, ve_c, range(h * share, (h + 1) * share))
+
+    ng, width, first, t_id = score_ids(nq, seq, kv, base)
 
     @pl.loop(0, nblk)
     def _(j):
@@ -125,30 +164,18 @@
             row = jnp.concatenate([vn_s[0, r, :], vn_s[1, r, :]], axis=-1)
             vbuf[slot, i, tt] = jnp.where(hit, row, vbuf[slot, i, tt].astype(F32)).astype(BF16)
 
-        parts = []
-        for g in range(groups):
+        def q_of(g):
             r = pl.ds(pl.multiple_of((j * groups + g) * ng, ng), ng)
-            qg = jnp.concatenate([q_s[0, r, :], q_s[1, r, :]], axis=-1).astype(BF16)
-            km = kbuf[slot, 2 * g:2 * g + 2].reshape(width, hd)
-            s = lax.dot_general(qg, km, (((1,), (1,)), ((), ())), preferred_element_type=F32)
-            s = SOFT_CAP * jnp.tanh(s * scale)
-            b = j * blk + 2 * g
-            lim = jnp.where(first, pos_s[b], pos_s[b + 1])
-            parts.append(jnp.where(t_id <= lim, s, NEG_FILL))
-        sc = jnp.concatenate(parts, axis=0)
-        m = jnp.max(sc, axis=-1, keepdims=True)
-        e = jnp.where(sc > 0.5 * NEG_FILL, jnp.exp(sc - m), 0.0)
-        l = jnp.sum(e, axis=-1, keepdims=True)
-        some = l > 0.0
-        inv = jnp.where(some, 1.0 / jnp.where(some, l, 1.0), 0.0)
-        p_s[...] = e.astype(BF16)
-        for g in range(groups):
-            vm = vbuf[slot, 2 * g:2 * g + 2].reshape(width, hd)
-            o = jnp.dot(p_s[g * ng:(g + 1) * ng, :], vm, preferred_element_type=F32)
-            o_ref[pl.ds(pl.multiple_of((j * groups + g) * ng, ng), ng), :] = o * inv[g * ng:(g + 1) * ng, :]
-        lse = jnp.where(some, m + jnp.log(jnp.where(some, l, 1.0)), NEG_FILL)
-        lse_t = jnp.broadcast_to(lse, (groups * ng, 128)).T
-        lse_ref[pl.ds(j, 1), :] = lse_t[0:1, :]
+            return jnp.concatenate([q_s[0, r, :], q_s[1, r, :]], axis=-1)
+
+        def lim_of(g):
+            return jnp.where(first, pos_s[j * blk + 2 * g], pos_s[j * blk + 2 * g + 1])
+
+        def put(g, o):
+            o_ref[pl.ds(pl.multiple_of((j * groups + g) * ng, ng), ng), :] = o
+
+        lse_ref[j] = attend(lambda g: kbuf[slot, 2 * g:2 * g + 2].reshape(width, hd), lambda g: vbuf[slot, 2 * g:2 * g + 2].reshape(width, hd),
+                            q_of, lim_of, put, groups, ng, t_id, p_s)
         k_o(j, slot).start()
         v_o(j, slot).start()
 
@@ -172,10 +199,14 @@
     return jnp.broadcast_to(row, (128, 128)).T
 
 
-def finish_kernel(cfg, o_ref, lse_ref, x_hbm, gain, wo_hbm, out_ref,
-                  x_ref, wo_v, r1, r1l, k2, k2l, s2, s2l, r2, r2l, wt, tmp, su, ku, ru, gat,
-                  l_sem, s_d1, r_d1, s_dl, r_dl, s_x, r_x, s_xl, r_xl, s_y, r_y, s_ax, r_ax, s_ay, r_ay, s_f, r_f, s_d2, r_d2):
-    nc, nq, hd = cfg
+def finish_kernel(cfg, pos_s, o_in, lse_in, q_c, ke_c, ve_c, x_hbm, gain, wo_hbm, kc, vc, out_ref, kv_buf,
+                  o_ref, lse_ref, p_s, x_ref, wo_v, r1, r1l, k2, k2l, s2, s2l, r2, r2l, wt, tmp, su, ku, ru, gat,
+                  l_sem, c_sem, s_d1, r_d1, s_dl, r_dl, s_x, r_x, s_xl, r_xl, s_y, r_y, s_ax, r_ax, s_ay, r_ay, s_f, r_f, s_d2, r_d2):
+    nc, nq, hd, early, blk = cfg
+    kbuf, vbuf = kv_buf.at[0], kv_buf.at[1]
+    seq, kv = kc.shape[1], kc.shape[2]
+    n_early, n_late = early // blk, kbuf.shape[0] // blk
+    span = blk * nq
     dp, tp, sp = lax.axis_index('dp'), lax.axis_index('tp'), lax.axis_index('sp')
     core, xx = lax.rem(sp, 2), sp // 2
     partner = (dp, tp, xx * 2 + 1 - core)
@@ -189,6 +220,24 @@
     x_load = pltpu.make_async_copy(x_hbm, x_ref, l_sem.at[1])
     wo_load.start()
     x_load.start()
+
+    def k_in(j):
+        return pltpu.make_async_copy(kc.at[pl.ds(early + j * blk, blk)], kbuf.at[pl.ds(j * blk, blk)], c_sem.at[0, j])
+
+    def v_in(j):
+        return pltpu.make_async_copy(vc.at[pl.ds(early + j * blk, blk)], vbuf.at[pl.ds(j * blk, blk)], c_sem.at[1, j])
+
+    @pl.loop(0, n_late)
+    def _(j):
+        k_in(j).start()
+        v_in(j).start()
+
+    @pl.loop(0, n_early)
+    def _(j):
+        r = pl.ds(pl.multiple_of(j * span, span), span)
+        o_ref[r, :] = o_in[r, :]
+        lse_ref[j] = lse_in[j]
+
     barrier = pltpu.get_barrier_semaphore()
     for dev in (partner, x_nbr, y_nbr):
         pl.semaphore_signal(barrier, inc=1, device_id=dev, device_id_type=MESH_ID)
@@ -198,7 +247,9 @@
         other = 2 * c + 1 - core
         return rcopy(o_ref.at[pl.ds(other * 128, 128)], r1.at[c], s_d1.at[c], r_d1.at[c], partner)
 
-    dl = rcopy(lse_ref, r1l, s_dl, r_dl, partner)
+    def dl(c):
+        other = 2 * c + 1 - core
+        return rcopy(lse_ref.at[other], r1l.at[other], s_dl.at[c], r_dl.at[c], partner)
 
     def xs(c):
         return rcopy(s2.at[c], r2.at[c], s_x.at[c], r_x.at[c], x_nbr)
@@ -209,37 +260,66 @@
     def ys(c):
         return rcopy(su.at[c], ru.at[c], s_y.at[c], r_y.at[c], y_nbr)
 
-    def blk(c, x, y):
+    def slab(c, x, y):
         return c * 8 + core * 4 + x * 2 + y
 
     def ag(c, sems, rsems, dev):
-        g = gat.at[blk(c, xx, tp)]
+        g = gat.at[slab(c, xx, tp)]
         return rcopy(g, g, sems.at[c], rsems.at[c], dev)
 
     def fw_y(c):
-        g = gat.at[blk(c, 1 - xx, tp)]
+        g = gat.at[slab(c, 1 - xx, tp)]
         return rcopy(g, g, s_f.at[c], r_f.at[c], y_nbr)
 
     def fw_x(c):
-        g = gat.at[blk(c, xx, 1 - tp)]
+        g = gat.at[slab(c, xx, 1 - tp)]
         return rcopy(g, g, s_f.at[c], r_f.at[c], x_nbr)
 
     def d2(c):
         g = gat.at[pl.ds(c * 8 + core * 4, 4)]
         return rcopy(g, g, s_d2.at[c], r_d2.at[c], partner)
 
-    dl.start()
-
-    @pl.loop(0, nc)
+    @pl.loop(0, n_early // 2)
     def _(c):
+        dl(c).start()
         d1(c).start()
 
-    dl.wait_recv()
+    ng, width, first, t_id = score_ids(nq, seq, kv, sp * seq)
+    groups = blk // 2
+
+    def stage_attend(j):
+        k_in(j).wait()
+        v_in(j).wait()
+        rows = pl.ds(pl.multiple_of(j * span, span), span)
+        at0 = pl.multiple_of(early * nq + j * span, span)
+        new = (q_c[0, rows, :], q_c[1, rows, :], ke_c[0, rows, :], ke_c[1, rows, :], ve_c[0, rows, :], ve_c[1, rows, :])
+
+        def q_of(g):
+            r = pl.ds(pl.multiple_of(j * span + g * ng, ng), ng)
+            return jnp.concatenate([q_c[0, r, :], q_c[1, r, :]], axis=-1)
+
+        def lim_of(g):
+            b = early + j * blk + 2 * g
+            return jnp.where(first, pos_s[b], pos_s[b + 1])
+
+        def put(g, o):
+            o_ref[pl.ds(pl.multiple_of(at0 + g * ng, ng), ng), :] = o
+
+        lse_ref[n_early + j] = attend(lambda g: kbuf[pl.ds(j * blk + 2 * g, 2)].reshape(width, hd),
+                                      lambda g: vbuf[pl.ds(j * blk + 2 * g, 2)].reshape(width, hd),
+                                      q_of, lim_of, put, groups, ng, t_id, p_s, new)
+
+        @pl.when(lax.rem(j, 2) == 1)
+        def _():
+            c = (n_early + j) // 2
+            dl(c).start()
+            d1(c).start()
 
     def stage_a(c):
         d1(c).wait_recv()
+        dl(c).wait_recv()
         mine = 2 * c + core
-        wa, wb, lse = merge_weights(lse_ref[pl.ds(mine, 1), :], r1l[pl.ds(mine, 1), :])
+        wa, wb, lse = merge_weights(lse_ref[mine], r1l[mine])
         wa, wb = columns(wa), columns(wb)
         r = pl.ds(pl.multiple_of(mine * 128, 128), 128)
         for i in range(hd // 128):
@@ -277,7 +357,7 @@
         u = ku[c] + ru[c]
         x = x_ref[pl.ds(pl.multiple_of(c * 64 + core * 32 + xx * 16, 16), 16), :].astype(F32)
         x = jnp.where(tp == 0, x[:8], x[8:])
-        gat[blk(c, xx, tp)] = x + rms_scale(u, gain[...])
+        gat[slab(c, xx, tp)] = x + rms_scale(u, gain[...])
         ag(c, s_ax, r_ax, x_nbr).start()
         ag(c, s_ay, r_ay, y_nbr).start()
 
@@ -332,11 +412,14 @@
         at(t, 8, stage_e)
         at(t, 9, stage_f)
 
-    dl.wait_send()
+        @pl.when(t < n_late)
+        def _():
+            stage_attend(t)
 
     @pl.loop(0, nc)
     def _(c):
         d1(c).wait_send()
+        dl(c).wait_send()
         xs(c).wait_send()
         xl(c).wait_send()
         ys(c).wait_send()
@@ -346,6 +429,39 @@
         d2(c).wait_send()
 
 
+def close_kernel(cfg, pos_s, x_ref, ke_c, ve_c, kv_in, k_part, v_part, x_out, k_out, v_out, kv_buf, x_sem, o_sem):
+    kb, vb = kv_buf.at[0], kv_buf.at[1]
+    early, blk, seq, nq, kv = cfg
+    base = lax.axis_index('sp') * seq
+    n_late = kb.shape[0] // blk
+    copy = pltpu.make_async_copy(x_ref, x_out, x_sem)
+    copy.start()
+
+    def out(i, buf, dst, j):
+        return pltpu.make_async_copy(buf.at[pl.ds(j * blk, blk)], dst.at[pl.ds(early + j * blk, blk)], o_sem.at[i, j])
+
+    @pl.loop(0, n_late)
+    def _(j):
+        for i in range(blk):
+            b = j * blk + i
+            t = pos_s[early + b] - base
+            hit = jnp.logical_and(t >= 0, t < seq)
+            tt = jnp.clip(t, 0, seq - 1)
+            r = pl.ds(nq * b, kv, stride=nq // kv)
+            for buf, new in ((kb, ke_c), (vb, ve_c)):
+                row = jnp.concatenate([new[0, r, :], new[1, r, :]], axis=-1)
+                buf[b, tt] = jnp.where(hit, row, buf[b, tt].astype(F32)).astype(BF16)
+        out(0, kb, k_out, j).start()
+        out(1, vb, v_out, j).start()
+
+    @pl.loop(0, n_late)
+    def _(j):
+        out(0, kb, k_out, j).wait()
+        out(1, vb, v_out, j).wait()
+
+    copy.wait()
+
+
 def solution(mesh):
     cache_spec = P('dp', 'sp', 'tp', None)
 
@@ -355,50 +471,68 @@
         nq = w_q.shape[1] // hd
         half = hd // 2
         blk, nbuf, lag = 32, 8, 3
-        nblk = rows // blk
+        late = 192
+        early = rows - late
+        nblk = early // blk
+        new_shape = pltpu.VMEM((2, late * nq, half), F32)
         inv_freq = (ROPE_BASE ** (-2.0 * np.arange(half) / hd)).astype(np.float32)[None, :]
         vmem, hbm = pl.BlockSpec(memory_space=pltpu.VMEM), pl.BlockSpec(memory_space=pl.ANY)
         dma = pltpu.SemaphoreType.DMA
-        cfg = (rows, seq, kv, hd, blk, nbuf, lag)
-        k_out, v_out, o_part, lse = pl.pallas_call(
+        cfg = (rows, early, seq, kv, hd, blk, nbuf, lag)
+        k_part, v_part, o_part, lse, q_c, ke_c, ve_c = pl.pallas_call(
             functools.partial(stream_kernel, cfg),
             name='stream',
             out_shape=[jax.ShapeDtypeStruct(k_cache.shape, BF16), jax.ShapeDtypeStruct(v_cache.shape, BF16),
-                       pltpu.VMEM((rows * nq, hd), F32), pltpu.VMEM((nblk, blk * nq), F32)],
+                       pltpu.VMEM((early * nq, hd), F32), pltpu.VMEM((nblk, 1, blk * nq), F32),
+                       new_shape, new_shape, new_shape],
             in_specs=[pl.BlockSpec(memory_space=pltpu.SMEM), vmem, vmem, hbm, vmem, hbm, hbm, hbm, hbm, hbm],
-            out_specs=[hbm, hbm, vmem, vmem],
+            out_specs=[hbm, hbm, vmem, vmem, vmem, vmem, vmem],
             scratch_shapes=[
                 pltpu.VMEM((rows, d_model), BF16),
                 pltpu.VMEM(w_q.shape, BF16), pltpu.VMEM(w_k.shape, BF16), pltpu.VMEM(w_v.shape, BF16),
                 pltpu.VMEM((2, rows, half), F32),
-                pltpu.VMEM((2, rows * nq, half), F32), pltpu.VMEM((2, rows * kv, half), F32), pltpu.VMEM((2, rows * kv, half), F32),
+                pltpu.VMEM((2, early * nq, half), F32), pltpu.VMEM((2, early * kv, half), F32), pltpu.VMEM((2, early * kv, half), F32),
                 pltpu.VMEM((nbuf, blk, seq, kv, hd), BF16), pltpu.VMEM((nbuf, blk, seq, kv, hd), BF16),
                 pltpu.VMEM((blk * nq, 2 * seq * kv), BF16),
                 dma((4,)), dma((nbuf,)), dma((nbuf,)), dma((nbuf,)), dma((nbuf,))],
-            compiler_params=pltpu.CompilerParams(vmem_limit_bytes=57_000_000),
+            compiler_params=pltpu.CompilerParams(vmem_limit_bytes=56_000_000),
             cost_estimate=pl.CostEstimate(flops=10 ** 10, bytes_accessed=150_000_000, transcendentals=0),
         )(cur_pos, cur_pos.reshape(rows // 128, 128), inv_freq, x_in, w_pre, w_q, w_k, w_v, k_cache, v_cache)
 
         nc, d_f32 = 8, (8, d_model)
-        x_out = pl.pallas_call(
-            functools.partial(finish_kernel, (nc, nq, hd)),
+        late_shape = pltpu.VMEM((2, late) + k_cache.shape[1:], BF16)
+        smem = pl.BlockSpec(memory_space=pltpu.SMEM)
+        x_new, kv_late = pl.pallas_call(
+            functools.partial(finish_kernel, (nc, nq, hd, early, blk)),
             name='finish',
-            out_shape=pltpu.VMEM(x_in.shape, BF16),
-            in_specs=[vmem, vmem, hbm, vmem, hbm],
-            out_specs=vmem,
+            out_shape=[pltpu.VMEM(x_in.shape, BF16), late_shape],
+            in_specs=[smem] + [vmem] * 5 + [hbm, vmem, hbm, hbm, hbm],
+            out_specs=[vmem, vmem],
             scratch_shapes=[
+                pltpu.VMEM((rows * nq, hd), F32), pltpu.VMEM((2 * nc, 1, 128), F32), pltpu.VMEM((blk * nq, 2 * seq * kv), BF16),
                 pltpu.VMEM(x_in.shape, BF16),
-                pltpu.VMEM(w_o.shape, BF16), pltpu.VMEM((nc, 128, hd), F32), pltpu.VMEM(lse.shape, F32),
+                pltpu.VMEM(w_o.shape, BF16), pltpu.VMEM((nc, 128, hd), F32), pltpu.VMEM((2 * nc, 1, 128), F32),
                 pltpu.VMEM((nc, hd // 128, 64, 128), F32), pltpu.VMEM((nc, 1, 128), F32),
                 pltpu.VMEM((nc, hd // 128, 64, 128), F32), pltpu.VMEM((nc, 1, 128), F32),
                 pltpu.VMEM((nc, hd // 128, 64, 128), F32), pltpu.VMEM((nc, 1, 128), F32),
                 pltpu.VMEM((2, 128, 128), F32), pltpu.VMEM((hd // 128, 128, 128), F32),
                 pltpu.VMEM((nc,) + d_f32, F32), pltpu.VMEM((nc,) + d_f32, F32), pltpu.VMEM((nc,) + d_f32, F32),
                 pltpu.VMEM((8 * nc,) + d_f32, F32),
-                dma((2,)), dma((nc,)), dma((nc,)), dma, dma] + [dma((nc,))] * 14,
-            compiler_params=pltpu.CompilerParams(vmem_limit_bytes=50_000_000, collective_id=0, has_side_effects=True),
+                dma((2,)), dma((2, late // blk))] + [dma((nc,))] * 18,
+            compiler_params=pltpu.CompilerParams(vmem_limit_bytes=24_000_000, collective_id=0, has_side_effects=True),
             cost_estimate=pl.CostEstimate(flops=10 ** 10, bytes_accessed=100_000_000, transcendentals=0),
-        )(o_part, lse, x_in, w_post, w_o)
+        )(cur_pos, o_part, lse, q_c, ke_c, ve_c, x_in, w_post, w_o, k_cache, v_cache)
+        x_out, k_out, v_out, _ = pl.pallas_call(
+            functools.partial(close_kernel, (early, blk, seq, nq, kv)),
+            name='close',
+            out_shape=[jax.ShapeDtypeStruct(x_in.shape, BF16), jax.ShapeDtypeStruct(k_cache.shape, BF16),
+                       jax.ShapeDtypeStruct(v_cache.shape, BF16), late_shape],
+            in_specs=[smem] + [vmem] * 4 + [hbm, hbm],
+            out_specs=[hbm, hbm, hbm, vmem],
+            input_output_aliases={4: 3, 5: 1, 6: 2},
+            scratch_shapes=[dma, dma((2, late // blk))],
+            compiler_params=pltpu.CompilerParams(vmem_limit_bytes=4_000_000),
+        )(cur_pos, x_new, ke_c, ve_c, kv_late, k_part, v_part)
         return x_out, k_out, v_out
 
     return jax.shard_map(local_step, mesh=mesh,

time: 95.3 us -> 91.6 us (0.961)
  Pallas kernels: 93.1 us -> 90.8 us
  local copies, waits for them, and re-layouts: 1.41 us -> 0.01 us
    pallas_call x1, Pallas kernels: 48.8 us -> 32.4 us  [local_step(): pl.pallas_call(functools.partial(stream_kernel, cfg), name='stream', out_...]
    pallas_call x1 -> x2, Pallas kernels: 44.3 us -> 58.4 us  [the longest x1 48.7 us: local_step(): pl.pallas_call(functools.partial(finish_kernel, (nc, nq, hd, early, blk))...]
    unnamed x3 -> x4, local copies, waits for them, and re-layouts: 1.41 us -> 0.01 us
where the time goes in v4:
time: 91.6 us; the launch traced here: 91.5 us
  Pallas kernels  90.8 us (99%)
    pallas_call x1, Pallas kernels, local_step(): pl.pallas_call(functools.partial(finish_kernel, (nc, nq, hd, early, blk))...  48.7 us
    pallas_call x1, Pallas kernels, local_step(): pl.pallas_call(functools.partial(stream_kernel, cfg), name='stream', out_...  32.4 us
    pallas_call x1, Pallas kernels, local_step(): pl.pallas_call(functools.partial(close_kernel, (early, blk, seq, nq, kv))...  9.78 us

profile of v4, /device:TPU:0, one launch (start us, length us, event | category | flops | bytes accessed | tf_op | source)
XLA Modules:
  0.0 91.5 jit_solution(17890203375215157748)
XLA Ops:
  0.6 0.0 copy-start
  0.6 0.0 copy-start.1
  0.7 32.4 %stream.1 = (bf16[512,64,2,256]{3,2,1,0:T(2,128)(2,1)}, bf16[512,64,2,256]{3,2,1,0:T(2,128)(2,1)}, f32[1280,256]{1,0:T(8,128)S(1)}, f32[10,1,128]{2,1,0:T(1,128)...) custom-call(s32[512]{0:T(512)} %pos_s.5, s32[4,128]{1,0:T(4,128)} %bitcast.1, ...), custom_call_target="tpu_custom_call" | custom-call | flops 10000000000 | bytes 150000000 | tf_op jit(solution)/shard_map/stream/pallas_call | solution.py:482
  33.0 0.0 copy-done
  33.0 0.0 copy-done.1
  33.0 48.7 %finish.1 = (bf16[512,2304]{1,0:T(8,128)(2,1)S(1)}, bf16[2,192,64,2,256]{4,3,2,1,0:T(2,128)(2,1)S(1)}) custom-call(s32[512]{0:T(512)S(1)} %copy-done, f32[1280,256]{1,0:T(8,128)S(1)} %get-tuple-element.15.o_in, f32[10,1,128]{2,1,0:T(1,128)S(1)} %get-tuple-element.16.lse_in, f32[2,768,128]{2,1,0:T(8,128)S(1)} %get-tuple-element.17.q_c, ...), custom_call_target="tpu_custom_call" | custom-call | flops 10000000000 | bytes 100000000 | tf_op jit(solution)/shard_map/finish/pallas_call | solution.py:505
  81.7 9.8 %close.1 = (bf16[512,2304]{1,0:T(8,128)(2,1)}, bf16[512,64,2,256]{3,2,1,0:T(2,128)(2,1)}, bf16[512,64,2,256]{3,2,1,0:T(2,128)(2,1)}, bf16[2,192,64,2,256]{4,3,2,1,0:T(2,128)(2,1)S(1)}) custom-call(s32[512]{0:T(512)S(1)} %copy-done, bf16[512,2304]{1,0:T(8,128)(2,1)S(1)} %get-tuple-element.20.x_ref, ...), custom_call_target="tpu_custom_call", output_to_operand_aliasing={{3}: (4, {}), {1}: (5, {}), {2}: (6, {})} | custom-call | tf_op jit(solution)/shard_map/close/pallas_call | solution.py:525
Async XLA Ops:
  0.6 32.4 %copy-start = (s32[512]{0:T(512)S(1)}, s32[512]{0:T(512)}, u32[]{:S(2)}) copy-start(s32[512]{0:T(512)} %pos_s.5) | copy-start | bytes 6148
  0.6 32.4 %copy-start.1 = (f32[2304]{0:T(1024)S(1)}, f32[2304]{0:T(1024)}, u32[]{:S(2)}) copy-start(f32[2304]{0:T(1024)} %gain.3) | copy-start | bytes 27652

commit v5 on v4

--- a/solution.py
+++ b/solution.py
@@ -216,6 +216,9 @@
     def rcopy(src, dst, ss, rs, dev):
         return pltpu.make_async_remote_copy(src_ref=src, dst_ref=dst, send_sem=ss, recv_sem=rs, device_id=dev, device_id_type=MESH_ID)
 
+    barrier = pltpu.get_barrier_semaphore()
+    for dev in (partner, x_nbr, y_nbr):
+        pl.semaphore_signal(barrier, inc=1, device_id=dev, device_id_type=MESH_ID)
     wo_load = pltpu.make_async_copy(wo_hbm, wo_v, l_sem.at[0])
     x_load = pltpu.make_async_copy(x_hbm, x_ref, l_sem.at[1])
     wo_load.start()
@@ -238,9 +241,6 @@
         o_ref[r, :] = o_in[r, :]
         lse_ref[j] = lse_in[j]
 
-    barrier = pltpu.get_barrier_semaphore()
-    for dev in (partner, x_nbr, y_nbr):
-        pl.semaphore_signal(barrier, inc=1, device_id=dev, device_id_type=MESH_ID)
     pl.semaphore_wait(barrier, 3)
 
     def d1(c):
@@ -399,6 +399,8 @@
 
     @pl.loop(0, nc + 9)
     def _(t):
+        at(t, 4, stage_c)
+        at(t, 6, stage_d)
         at(t, 0, stage_a)
 
         @pl.when(t == 2)
@@ -407,14 +409,12 @@
             x_load.wait()
 
         at(t, 2, stage_b)
-        at(t, 4, stage_c)
-        at(t, 6, stage_d)
         at(t, 8, stage_e)
         at(t, 9, stage_f)
 
-        @pl.when(t < n_late)
-        def _():
-            stage_attend(t)
+        @pl.when(jnp.logical_and(t >= 1, t <= n_late))
+        def _():
+            stage_attend(t - 1)
 
     @pl.loop(0, nc)
     def _(c):

time: 91.6 us -> 90 us (0.983)
  Pallas kernels: 90.8 us -> 89.1 us
    pallas_call x1, Pallas kernels: 48.7 us -> 47 us  [local_step(): pl.pallas_call(functools.partial(finish_kernel, (nc, nq, hd, early, blk))...]
where the time goes in v5:
time: 90 us; the launch traced here: 89.8 us
  Pallas kernels  89.1 us (99%)
    pallas_call x1, Pallas kernels, local_step(): pl.pallas_call(functools.partial(finish_kernel, (nc, nq, hd, early, blk))...  47 us
    pallas_call x1, Pallas kernels, local_step(): pl.pallas_call(functools.partial(stream_kernel, cfg), name='stream', out_...  32.4 us
    pallas_call x1, Pallas kernels, local_step(): pl.pallas_call(functools.partial(close_kernel, (early, blk, seq, nq, kv))...  9.78 us

profile of v5, /device:TPU:0, one launch (start us, length us, event | category | flops | bytes accessed | tf_op | source)
XLA Modules:
  0.0 89.8 jit_solution(9932736152610596670)
XLA Ops:
  0.6 0.0 copy-start
  0.6 0.0 copy-start.1
  0.7 32.4 %stream.1 = (bf16[512,64,2,256]{3,2,1,0:T(2,128)(2,1)}, bf16[512,64,2,256]{3,2,1,0:T(2,128)(2,1)}, f32[1280,256]{1,0:T(8,128)S(1)}, f32[10,1,128]{2,1,0:T(1,128)...) custom-call(s32[512]{0:T(512)} %pos_s.5, s32[4,128]{1,0:T(4,128)} %bitcast.1, ...), custom_call_target="tpu_custom_call" | custom-call | flops 10000000000 | bytes 150000000 | tf_op jit(solution)/shard_map/stream/pallas_call | solution.py:482
  33.0 0.0 copy-done
  33.0 0.0 copy-done.1
  33.0 47.0 %finish.1 = (bf16[512,2304]{1,0:T(8,128)(2,1)S(1)}, bf16[2,192,64,2,256]{4,3,2,1,0:T(2,128)(2,1)S(1)}) custom-call(s32[512]{0:T(512)S(1)} %copy-done, f32[1280,256]{1,0:T(8,128)S(1)} %get-tuple-element.15.o_in, f32[10,1,128]{2,1,0:T(1,128)S(1)} %get-tuple-element.16.lse_in, f32[2,768,128]{2,1,0:T(8,128)S(1)} %get-tuple-element.17.q_c, ...), custom_call_target="tpu_custom_call" | custom-call | flops 10000000000 | bytes 100000000 | tf_op jit(solution)/shard_map/finish/pallas_call | solution.py:505
  80.0 9.8 %close.1 = (bf16[512,2304]{1,0:T(8,128)(2,1)}, bf16[512,64,2,256]{3,2,1,0:T(2,128)(2,1)}, bf16[512,64,2,256]{3,2,1,0:T(2,128)(2,1)}, bf16[2,192,64,2,256]{4,3,2,1,0:T(2,128)(2,1)S(1)}) custom-call(s32[512]{0:T(512)S(1)} %copy-done, bf16[512,2304]{1,0:T(8,128)(2,1)S(1)} %get-tuple-element.20.x_ref, ...), custom_call_target="tpu_custom_call", output_to_operand_aliasing={{3}: (4, {}), {1}: (5, {}), {2}: (6, {})} | custom-call | tf_op jit(solution)/shard_map/close/pallas_call | solution.py:525
Async XLA Ops:
  0.6 32.4 %copy-start = (s32[512]{0:T(512)S(1)}, s32[512]{0:T(512)}, u32[]{:S(2)}) copy-start(s32[512]{0:T(512)} %pos_s.5) | copy-start | bytes 6148
  0.6 32.4 %copy-start.1 = (f32[2304]{0:T(1024)S(1)}, f32[2304]{0:T(1024)}, u32[]{:S(2)}) copy-start(f32[2304]{0:T(1024)} %gain.3) | copy-start | bytes 27652

commit v6 on v5

--- a/solution.py
+++ b/solution.py
@@ -470,7 +470,7 @@
         d_model = x_in.shape[1]
         nq = w_q.shape[1] // hd
         half = hd // 2
-        blk, nbuf, lag = 32, 8, 3
+        blk, nbuf, lag = 32, 8, 2
         late = 192
         early = rows - late
         nblk = early // blk

time: 90 us -> 89.9 us (level)
  no operation moved by 1% of the time
where the time goes in v6:
time: 89.9 us; the launch traced here: 89.8 us
  Pallas kernels  89.1 us (99%)
    pallas_call x1, Pallas kernels, local_step(): pl.pallas_call(functools.partial(finish_kernel, (nc, nq, hd, early, blk))...  47 us
    pallas_call x1, Pallas kernels, local_step(): pl.pallas_call(functools.partial(stream_kernel, cfg), name='stream', out_...  32.3 us
    pallas_call x1, Pallas kernels, local_step(): pl.pallas_call(functools.partial(close_kernel, (early, blk, seq, nq, kv))...  9.78 us

profile of v6, /device:TPU:0, one launch (start us, length us, event | category | flops | bytes accessed | tf_op | source)
XLA Modules:
  0.0 89.8 jit_solution(12991020181055190448)
XLA Ops:
  0.6 0.0 copy-start
  0.6 0.0 copy-start.1
  0.7 32.3 %stream.1 = (bf16[512,64,2,256]{3,2,1,0:T(2,128)(2,1)}, bf16[512,64,2,256]{3,2,1,0:T(2,128)(2,1)}, f32[1280,256]{1,0:T(8,128)S(1)}, f32[10,1,128]{2,1,0:T(1,128)...) custom-call(s32[512]{0:T(512)} %pos_s.5, s32[4,128]{1,0:T(4,128)} %bitcast.1, ...), custom_call_target="tpu_custom_call" | custom-call | flops 10000000000 | bytes 150000000 | tf_op jit(solution)/shard_map/stream/pallas_call | solution.py:482
  33.0 0.0 copy-done
  33.0 0.0 copy-done.1
  33.0 47.0 %finish.1 = (bf16[512,2304]{1,0:T(8,128)(2,1)S(1)}, bf16[2,192,64,2,256]{4,3,2,1,0:T(2,128)(2,1)S(1)}) custom-call(s32[512]{0:T(512)S(1)} %copy-done, f32[1280,256]{1,0:T(8,128)S(1)} %get-tuple-element.15.o_in, f32[10,1,128]{2,1,0:T(1,128)S(1)} %get-tuple-element.16.lse_in, f32[2,768,128]{2,1,0:T(8,128)S(1)} %get-tuple-element.17.q_c, ...), custom_call_target="tpu_custom_call" | custom-call | flops 10000000000 | bytes 100000000 | tf_op jit(solution)/shard_map/finish/pallas_call | solution.py:505
  80.0 9.8 %close.1 = (bf16[512,2304]{1,0:T(8,128)(2,1)}, bf16[512,64,2,256]{3,2,1,0:T(2,128)(2,1)}, bf16[512,64,2,256]{3,2,1,0:T(2,128)(2,1)}, bf16[2,192,64,2,256]{4,3,2,1,0:T(2,128)(2,1)S(1)}) custom-call(s32[512]{0:T(512)S(1)} %copy-done, bf16[512,2304]{1,0:T(8,128)(2,1)S(1)} %get-tuple-element.20.x_ref, ...), custom_call_target="tpu_custom_call", output_to_operand_aliasing={{3}: (4, {}), {1}: (5, {}), {2}: (6, {})} | custom-call | tf_op jit(solution)/shard_map/close/pallas_call | solution.py:525
Async XLA Ops:
  0.6 32.4 %copy-start = (s32[512]{0:T(512)S(1)}, s32[512]{0:T(512)}, u32[]{:S(2)}) copy-start(s32[512]{0:T(512)} %pos_s.5) | copy-start | bytes 6148
  0.6 32.4 %copy-start.1 = (f32[2304]{0:T(1024)S(1)}, f32[2304]{0:T(1024)}, u32[]{:S(2)}) copy-start(f32[2304]{0:T(1024)} %gain.3) | copy-start | bytes 27652
